TPU v7x, 128 devices: a whole 4x4x4 slice. The times are simulated.
128 devices in a mesh: dp: 1, dcp: 128 (over z, y, x, core).
Axes of the slice: x: 4, y: 4, z: 4, core: 2. Of those that a mesh axis runs over, the one named last changes fastest.
Arguments:
- q_abs: bfloat16 [64, 2, 128, 576], P('dp', None, 'dcp')
- kv_cache: bfloat16 [64, 2, 128, 64, 576], P('dp', None, 'dcp')
- lengths: int32 [64], P('dp')
Outputs:
- output: bfloat16 [64, 2, 128, 512], P('dp', None, 'dcp')
All inputs are finite; a program needn't handle non-finite values.
Results may differ from a plain program's by a relative error of at most 0.00650124.
Values are sent between devices in bfloat16 or wider.
A program may use at most 1 GiB of HBM per device.

v0:
```python
import jax
import jax.numpy as jnp
from jax import lax
from jax.sharding import PartitionSpec as P

LATENT = 512
ROPE = 64
NOPE = 128
PAGE = 64
MASKED = -1e30


def solution(mesh):
    group_size = mesh.shape['dcp']
    score_scale = (NOPE + ROPE) ** -0.5

    def local_step(q_blk, kv_blk, len_blk):
        batch_loc, tok_count, heads_loc, q_width = q_blk.shape
        rounds = kv_blk.shape[1]
        local_keys = kv_blk.reshape(batch_loc, rounds * PAGE, q_width)
        q_all = lax.all_gather(q_blk, 'dcp', axis=2, tiled=True)
        scores = jnp.einsum('bthd,bsd->bths', q_all, local_keys, preferred_element_type=jnp.float32) * score_scale
        device = lax.axis_index('dcp')
        positions = ((jnp.arange(rounds)[:, None] * group_size + device) * PAGE + jnp.arange(PAGE)[None, :]).reshape(rounds * PAGE)
        last_pos = len_blk[:, None] - tok_count + jnp.arange(tok_count)[None, :]
        visible = positions[None, None, None, :] <= last_pos[:, :, None, None]
        scores = jnp.where(visible, scores, MASKED)
        row_max = jnp.max(scores, axis=-1)
        weights = jnp.exp(scores - row_max[..., None])
        row_sum = jnp.sum(weights, axis=-1)
        part_out = jnp.einsum('bths,bsc->bthc', weights.astype(jnp.bfloat16), local_keys[:, :, :LATENT], preferred_element_type=jnp.float32)
        part_out = (part_out / row_sum[..., None]).astype(jnp.bfloat16)
        part_lse = row_max + jnp.log(row_sum)
        recv_out = lax.all_to_all(part_out, 'dcp', 2, 2, tiled=True).reshape(batch_loc, tok_count, group_size, heads_loc, LATENT)
        recv_lse = lax.all_to_all(part_lse, 'dcp', 2, 2, tiled=True).reshape(batch_loc, tok_count, group_size, heads_loc)
        total_lse = jax.nn.logsumexp(recv_lse, axis=2, keepdims=True)
        merge_w = jnp.exp(recv_lse - total_lse)
        merged = jnp.sum(merge_w[..., None] * recv_out.astype(jnp.float32), axis=2)
        return merged.astype(jnp.bfloat16)

    return jax.shard_map(local_step, mesh=mesh, in_specs=(P('dp', None, 'dcp', None), P('dp', None, 'dcp', None, None), P('dp')), out_specs=P('dp', None, 'dcp', None), check_vma=False)
```

profile of v0, /device:TPU:11, one launch (start us, length us, event | category | flops | bytes accessed | tf_op | source)
XLA Modules:
  0.0 469.2 jit_solution(11272095565451875131)
XLA Ops:
  6.5 0.0 all-gather.2.cloned.1.call-start
  6.5 1.6 copy.21
  8.1 0.0 all-gather.2.cloned.1.call-update
  8.2 0.1 iota_add_fusion.1
  8.2 0.1 add.66
  8.3 0.7 broadcast_add_fusion
  9.0 0.1 iota_add_fusion
  9.1 0.1 broadcast_compare_fusion
  9.2 90.5 %all-gather.2.cloned.1.call-done = bf16[64,2,128,576]{3,0,1,2:T(8,128)(2,1)} async-done(((bf16[64,2,1,576]{3,0,1,2:T(8,128)(2,1)}), bf16[64,2,128,576]{3,0,1,2:T(8,128)(2,1)}) %all-gather.2.cloned.1.call-update) | async-done | bytes 18874384 | tf_op jit(solution)/shard_map/all_gather | solution.py:21
  99.7 16.6 %fusion.3 = (f32[64,2,128]{2,1,0:T(2,128)S(1)}, f32[64,2,128,128]{2,3,1,0:T(8,128)S(1)}) fusion(pred[64,2,128]{2,1,0:T(4,128)(4,1)S(1)} %broadcast_compare_fusion, bf16[64,128,576,1]{2,1,3,0:T(8,128)(2,1)} %bitcast.22, bf16[64,2,128,576]{3,0,1,2:T(8,128)(2,1)} %all-gather.2.cloned.1.call-done), kind=kOutput, calls=%fused_computation.8 | convolution fusion | flops 2422194176 | bytes 36782080 | tf_op jit(solution)/shard_map/bthd,bsd->bths/dot_general | solution.py:22
  116.3 0.0 copy-start
  116.3 3.2 copy-done
  119.5 3.1 fusion.5
  122.7 0.1 copy.26
  122.8 0.8 reshape.113
  123.6 7.5 %all-to-all-start = ((f32[128,1,128]{2,1,0:T(1,128)}), f32[128,1,128]{2,1,0:T(1,128)S(1)}, u32[]{:S(2)}, u32[]{:S(2)}) async-start(f32[128,1,128]{2,1,0:T(1,128)} %reshape.113), calls=%async_computation | async-start | bytes 131072 | tf_op jit(solution)/shard_map/all_to_all | solution.py:35
  131.0 11.2 %divide_convert_fusion = bf16[64,2,128,512]{3,2,1,0:T(8,128)(2,1)S(1)} fusion(f32[64,2,128]{2,1,0:T(2,128)S(1)} %fusion.5, bf16[64,128,576]{2,1,0:T(8,128)(2,1)} %bitcast.23, f32[64,2,128,128]{2,3,1,0:T(8,128)} %copy-done, f32[64,2,128]{2,1,0:T(2,128)S(1)} %get-tuple-element.5, pred[64,2,128]{2,1,0:T(4,128)(4,1)S(1)} %broadcast_compare_fusion), kind=kOutput, calls=%fused_computation.1 | convolution fusion | flops 2172649472 | bytes 33701888 | tf_op jit(solution)/shard_map/bths,bsc->bthc/dot_general | solution.py:31
  142.2 35.7 %copy.30 = bf16[64,2,128,512]{3,1,0,2:T(2,128)(2,1)} copy(bf16[64,2,128,512]{3,2,1,0:T(8,128)(2,1)S(1)} %divide_convert_fusion) | data formatting | bytes 33554432 | tf_op jit(solution)/shard_map/convert_element_type | solution.py:32
  177.9 0.0 all-to-all-done
  177.9 10.2 %all-to-all-start.1 = ((bf16[64,2,128,512]{3,1,0,2:T(2,128)(2,1)}), bf16[64,2,128,512]{3,1,0,2:T(2,128)(2,1)}, u32[]{:S(2)}, u32[]{:S(2)}) async-start(bf16[64,2,128,512]{3,1,0,2:T(2,128)(2,1)} %copy.30), calls=%async_computation.1 | async-start | bytes 33554432 | tf_op jit(solution)/shard_map/all_to_all | solution.py:34
  188.1 0.5 broadcast.78
  188.6 0.8 reduce.6
  189.4 0.1 reshape.114
  189.6 0.1 copy.27
  189.6 0.2 bitcast_reduce_fusion
  189.8 0.2 exponential_reduce_fusion
  190.0 0.1 subtract_exponential_fusion.1
  190.1 4.5 copy.28
  194.6 245.3 %all-to-all-done.1 = bf16[64,2,128,512]{3,1,0,2:T(2,128)(2,1)} async-done(((bf16[64,2,128,512]{3,1,0,2:T(2,128)(2,1)}), bf16[64,2,128,512]{3,1,0,2:T(2,128)(2,1)}, u32[]{:S(2)}, u32[]{:S(2)}) %all-to-all-start.1) | async-done | bytes 16777248 | tf_op jit(solution)/shard_map/all_to_all | solution.py:34
  439.9 22.4 %multiply_reduce_fusion = bf16[64,2,512]{2,1,0:T(2,128)(2,1)} fusion(bf16[64,2,128,512]{3,1,0,2:T(2,128)(2,1)} %all-to-all-done.1, f32[64,2,128]{1,0,2:T(8,128)} %copy.28), kind=kLoop, calls=%fused_computation | loop fusion | flops 25100288 | bytes 16973824 | tf_op jit(solution)/shard_map/reduce_sum | solution.py:38
  (4 shorter events, 0.0 us)
Async XLA Ops:
  6.5 93.1 %all-gather.2.cloned.1.call-start = ((), (), s32[]{:S(2)}) async-start(), calls=%async_computation.2 | async-start | bytes 21135360 | tf_op jit(solution)/shard_map/all_gather | solution.py:21
  116.3 3.2 copy-start
  123.6 54.3 %all-to-all-start = ((f32[128,1,128]{2,1,0:T(1,128)}), f32[128,1,128]{2,1,0:T(1,128)S(1)}, u32[]{:S(2)}, u32[]{:S(2)}) async-start(f32[128,1,128]{2,1,0:T(1,128)} %reshape.113), calls=%async_computation | async-start | bytes 131072 | tf_op jit(solution)/shard_map/all_to_all | solution.py:35
  177.9 262.0 %all-to-all-start.1 = ((bf16[64,2,128,512]{3,1,0,2:T(2,128)(2,1)}), bf16[64,2,128,512]{3,1,0,2:T(2,128)(2,1)}, u32[]{:S(2)}, u32[]{:S(2)}) async-start(bf16[64,2,128,512]{3,1,0,2:T(2,128)(2,1)} %copy.30), calls=%async_computation.1 | async-start | bytes 33554432 | tf_op jit(solution)/shard_map/all_to_all | solution.py:34
Sparse Core Ops, SparseCore 0:
  10.3 89.3 all-gather.1
where the time goes:
time: 469 us
  waiting for transfers between devices  336 us (72%)
  local copies, waits for them, and re-layouts  46.7 us (10%)
  matrix products  27.8 us (6%)
  other arithmetic  27.7 us (6%)
  starting transfers between devices  17.7 us (4%)
  between operations  13.5 us (3%)
    all_to_all x1, waiting for transfers between devices, local_step(): lax.all_to_all(part_out, 'dcp', 2, 2, tiled=True)  245 us
    all_gather x1, waiting for transfers between devices, local_step(): q_all = lax.all_gather(q_blk, 'dcp', axis=2, tiled=True)  90.5 us
    convert_element_type x1, local copies, waits for them, and re-layouts, local_step(): part_out = (part_out / row_sum[..., None]).astype(jnp.bfloat16)  35.7 us
    reduce_sum x1, other arithmetic, local_step(): merged = jnp.sum(merge_w[..., None] * recv_out.astype(jnp.float32), axis=2)  22.4 us
    dot_general x1, matrix products, local_step(): jnp.einsum('bthd,bsd->bths', q_all, local_keys, preferred_element_type=jn...  16.6 us
    dot_general x1, matrix products, local_step(): jnp.einsum('bths,bsc->bthc', weights.astype(jnp.bfloat16), local_keys[:,...  11.2 us
    all_to_all x1, starting transfers between devices, local_step(): lax.all_to_all(part_out, 'dcp', 2, 2, tiled=True)  10.2 us
  transfers between devices with their start and end apart: 3, of which 2 were waited for; matrix products, arithmetic and copies ran while one was open for 12% of the time, Pallas kernels for 0%

commit v1 on v0

v1 whole, which is shorter than its diff:
```python
import jax
import jax.numpy as jnp
from jax import lax
from jax.experimental import pallas as pl
from jax.experimental.pallas import tpu as pltpu
from jax.sharding import PartitionSpec as P

LATENT = 512
ROPE = 64
NOPE = 128
WIDTH = LATENT + ROPE
PAGE = 64
GROUP = 128
BATCH = 64
MASKED = -1e30
SCALE = (NOPE + ROPE) ** -0.5
MESH = pl.DeviceIdType.MESH

SZ, SY, SX = 32, 8, 2
RING = (SZ, SY, SX)
AX1 = (SY, SZ, SZ)
AX2 = (SX, SX, SY)
COUNT = (3, 3, 2)
BASE = (0, 24, 48)
SLOTS = 8


def pick(k, vals):
    return jnp.where(k == 0, vals[0], jnp.where(k == 1, vals[1], vals[2]))


def coord(me, stride):
    return lax.rem(lax.div(me, stride), 4)


def shifted(me, stride, d):
    c = coord(me, stride)
    return me + (lax.rem(c + d, 4) - c) * stride


def remote(src, dst, ssem, rsem, dev):
    return pltpu.make_async_remote_copy(src_ref=src, dst_ref=dst, send_sem=ssem, recv_sem=rsem, device_id={'dcp': dev}, device_id_type=MESH)


def kernel(len_ref, q_ref, kv_ref, out_ref, kvbuf, q0buf, qbuf, obuf, rsbuf, lbuf, lrecv, fsend, frecv,
           kv_s, kv_r, kv_l, q0_s, q0_r, q1_s, q1_r, q2_s, q2_r, rs_s, rs_r, l_s, l_r, f_s, f_r):
    me = lax.axis_index('dcp')
    core = lax.rem(me, 2)
    cx, cy, cz = coord(me, SX), coord(me, SY), coord(me, SZ)
    del cx, cy, cz

    bar = pltpu.get_barrier_semaphore()
    peers = [me + 1 - 2 * core]
    for s in (SZ, SY, SX):
        for d in (1, 2, 3):
            t = shifted(me, s, d)
            peers += [t, t + 1 - 2 * core]
    for s1, s2 in ((SZ, SY), (SZ, SX), (SY, SX)):
        for d1 in (1, 2, 3):
            for d2 in (1, 2, 3):
                peers.append(shifted(shifted(me, s1, d1), s2, d2))
    for t in peers:
        pl.semaphore_signal(bar, inc=1, device_id={'dcp': t}, device_id_type=MESH)
    lbuf[...] = jnp.zeros_like(lbuf)
    pl.semaphore_wait(bar, len(peers))

    own = [coord(me, RING[k]) * 2 + core for k in range(3)]

    def ring_dest(k, d, flip):
        dev = shifted(me, RING[k], d)
        dcore = core
        if flip:
            dev = dev + 1 - 2 * core
            dcore = 1 - core
        return dev, coord(dev, RING[k]) * 2 + dcore

    others = [(1, 0), (3, 0), (2, 0), (1, 1), (3, 1), (2, 1), (0, 1)]

    for k in range(3):
        for d, flip in others:
            dev, o = ring_dest(k, d, flip)
            remote(q_ref.at[k, o], q0buf.at[k, own[k]], q0_s.at[k], q0_r.at[k], dev).start()
        q0buf[k, own[k]] = q_ref[k, own[k]]

    def send_cache(t):
        k, i = t % 3, t // 3
        pltpu.make_async_copy(kv_ref.at[BASE[k] + own[k] * COUNT[k] + i, :, 0], kvbuf.at[t, own[k]], kv_l.at[t]).start()
        for d, flip in others:
            dev, o = ring_dest(k, d, flip)
            remote(kv_ref.at[BASE[k] + o * COUNT[k] + i, :, 0], kvbuf.at[t, own[k]], kv_s.at[t], kv_r.at[t], dev).start()

    for t in range(0, 3):
        send_cache(t)

    place = [coord(me, AX2[k]) * 4 + coord(me, AX1[k]) for k in range(3)]
    for k in range(3):
        n = COUNT[k]
        remote(q_ref.at[k, pl.ds(0, 7)], q0buf.at[k, pl.ds(0, 7)], q0_s.at[k], q0_r.at[k], me).wait_recv()
        row = lax.broadcasted_iota(jnp.int32, (n * 16, 128), 0)
        col = lax.broadcasted_iota(jnp.int32, (n * 16, 128), 1)
        want = (((row & 15) >> 1) << 4) + ((row >> 4) << 1) + (row & 1)
        perm = jnp.where(col == want, 1.0, 0.0).astype(jnp.bfloat16)
        rows = q0buf[k].reshape(128, WIDTH)
        piece = jnp.dot(perm, rows, preferred_element_type=jnp.float32).astype(jnp.bfloat16)
        qbuf[k, pl.ds(0, n), place[k]] = piece.reshape(n, 16, WIDTH)
        for d in (1, 3, 2):
            view = qbuf.at[k, pl.ds(0, n), place[k]]
            remote(view, view, q1_s.at[k], q1_r.at[k], shifted(me, AX1[k], d)).start()

    for t in range(3, 6):
        send_cache(t)

    for k in range(3):
        n = COUNT[k]
        three = qbuf.at[k, pl.ds(0, n), pl.ds(0, 3)]
        remote(three, three, q1_s.at[k], q1_r.at[k], me).wait_recv()
        view = qbuf.at[k, pl.ds(0, n), pl.ds(coord(me, AX2[k]) * 4, 4)]
        for d in (1, 3, 2):
            remote(view, view, q2_s.at[k], q2_r.at[k], shifted(me, AX2[k], d)).start()

    for t in range(6, SLOTS):
        send_cache(t)

    for k in range(3):
        n = COUNT[k]
        twelve = qbuf.at[k, pl.ds(0, n), pl.ds(0, 12)]
        remote(twelve, twelve, q2_s.at[k], q2_r.at[k], me).wait_recv()

    def attend(t, carry):
        k = lax.rem(t, 3)
        i = lax.div(t, 3)
        ring = pick(k, RING)
        u = coord(me, ring)
        o_me = u * 2 + core
        c1 = coord(me, pick(k, AX1))
        c2 = coord(me, pick(k, AX2))
        p_me = c2 * 4 + c1
        seq = 24 * k + o_me * pick(k, COUNT) + i
        length = len_ref[seq]
        pltpu.make_async_copy(kv_ref.at[0, :, 0], kvbuf.at[t, 0], kv_l.at[t]).wait()
        remote(kv_ref.at[pl.ds(0, 7), :, 0], kvbuf.at[t, pl.ds(0, 7)], kv_s.at[t], kv_r.at[t], me).wait_recv()
        q = qbuf[k, i].reshape(256, WIDTH)
        keys = kvbuf[t].reshape(1024, WIDTH)
        nt = (((1,), (1,)), ((), ()))
        s = lax.dot_general(q[:, :LATENT], keys[:, :LATENT], nt, preferred_element_type=jnp.float32)
        s = s + lax.dot_general(q[:, LATENT:], keys[:, LATENT:], nt, preferred_element_type=jnp.float32)
        s = s * SCALE
        kk = lax.broadcasted_iota(jnp.int32, (1, 1024), 1)
        dsrc = (me - u * ring - core) + (kk >> 8) * ring + ((kk >> 7) & 1)
        pos = (((kk >> 6) & 1) * GROUP + dsrc) * PAGE + (kk & 63)
        tok = lax.broadcasted_iota(jnp.int32, (256, 1), 0) & 1
        s = jnp.where(pos - tok <= length - 2, s, MASKED)
        m = jnp.max(s, axis=1, keepdims=True)
        w = jnp.exp(s - m)
        l = jnp.sum(w, axis=1, keepdims=True)
        part = jnp.dot(w.astype(jnp.bfloat16), keys[:, :LATENT], preferred_element_type=jnp.float32)
        part = (part * (1.0 / l)).astype(jnp.bfloat16)
        obuf[k, i] = part.reshape(16, 16, LATENT)
        lse = m + jnp.log(l)
        hi = lse.astype(jnp.bfloat16).astype(jnp.float32)
        mid = (lse - hi).astype(jnp.bfloat16).astype(jnp.float32)
        lo = lse - hi - mid
        lane = lax.broadcasted_iota(jnp.int32, (256, 128), 1)
        old = lbuf[k].reshape(256, 128).astype(jnp.float32)
        new = jnp.where(lane == i, hi, jnp.where(lane == 8 + i, mid, jnp.where(lane == 16 + i, lo, old)))
        lbuf[k] = new.astype(jnp.bfloat16).reshape(16, 16, 128)

        def dest(d1, d2):
            e1, e2 = lax.rem(c1 + d1, 4), lax.rem(c2 + d2, 4)
            return me + (e1 - c1) * pick(k, AX1) + (e2 - c2) * pick(k, AX2), e2 * 4 + e1

        order = [(d1, d2) for d1 in range(4) for d2 in range(4) if d1 or d2]
        for d1, d2 in order:
            dev, p = dest(d1, d2)
            remote(obuf.at[k, i, p], rsbuf.at[k, i, p_me], rs_s.at[t], rs_r.at[t], dev).start()
        rsbuf[k, i, p_me] = obuf[k, i, p_me]

        @pl.when(t >= 5)
        def _():
            for d1, d2 in order:
                dev, p = dest(d1, d2)
                remote(lbuf.at[k, p], lrecv.at[k, p_me], l_s.at[k], l_r.at[k], dev).start()
            lrecv[k, p_me] = lbuf[k, p_me]

        return carry

    lax.fori_loop(0, SLOTS, attend, 0)

    for k in (2, 0, 1):
        n = COUNT[k]
        remote(lbuf.at[k, pl.ds(0, 15)], lrecv.at[k, pl.ds(0, 15)], l_s.at[k], l_r.at[k], me).wait_recv()
        lr = lrecv[k].astype(jnp.float32)
        merged = []
        for i in range(n):
            t = 3 * i + k
            remote(obuf.at[k, i, pl.ds(0, 15)], rsbuf.at[k, i, pl.ds(0, 15)], rs_s.at[t], rs_r.at[t], me).wait_recv()
            lse = lr[:, :, i:i + 1] + lr[:, :, 8 + i:9 + i] + lr[:, :, 16 + i:17 + i]
            top = jnp.max(lse, axis=0, keepdims=True)
            e = jnp.exp(lse - top)
            wgt = e / jnp.sum(e, axis=0, keepdims=True)
            acc = wgt[0] * rsbuf[k, i, 0].astype(jnp.float32)
            for p in range(1, 16):
                acc = acc + wgt[p] * rsbuf[k, i, p].astype(jnp.float32)
            merged.append(acc.astype(jnp.bfloat16))
        rows = jnp.concatenate(merged, axis=0)
        row = lax.broadcasted_iota(jnp.int32, (128, n * 16), 0)
        col = lax.broadcasted_iota(jnp.int32, (128, n * 16), 1)
        have = (((col & 15) >> 1) << 4) + ((col >> 4) << 1) + (col & 1)
        perm = jnp.where(row == have, 1.0, 0.0).astype(jnp.bfloat16)
        fsend[k] = jnp.dot(perm, rows, preferred_element_type=jnp.float32).astype(jnp.bfloat16).reshape(8, 16, LATENT)
        for d, flip in others:
            dev, o = ring_dest(k, d, flip)
            remote(fsend.at[k, o], frecv.at[k, own[k]], f_s.at[k], f_r.at[k], dev).start()
        frecv[k, own[k]] = fsend[k, own[k]]

    for k in (2, 0, 1):
        remote(fsend.at[k, pl.ds(0, 7)], frecv.at[k, pl.ds(0, 7)], f_s.at[k], f_r.at[k], me).wait_recv()
        out_ref[k] = frecv[k]

    for t in range(SLOTS):
        k, i = t % 3, t // 3
        remote(kv_ref.at[pl.ds(0, 7), :, 0], kvbuf.at[t, pl.ds(0, 7)], kv_s.at[t], kv_r.at[t], me).wait_send()
        remote(obuf.at[k, i, pl.ds(0, 15)], rsbuf.at[k, i, pl.ds(0, 15)], rs_s.at[t], rs_r.at[t], me).wait_send()
    for k in range(3):
        n = COUNT[k]
        remote(q_ref.at[k, pl.ds(0, 7)], q0buf.at[k, pl.ds(0, 7)], q0_s.at[k], q0_r.at[k], me).wait_send()
        three = qbuf.at[k, pl.ds(0, n), pl.ds(0, 3)]
        remote(three, three, q1_s.at[k], q1_r.at[k], me).wait_send()
        twelve = qbuf.at[k, pl.ds(0, n), pl.ds(0, 12)]
        remote(twelve, twelve, q2_s.at[k], q2_r.at[k], me).wait_send()
        remote(lbuf.at[k, pl.ds(0, 15)], lrecv.at[k, pl.ds(0, 15)], l_s.at[k], l_r.at[k], me).wait_send()
        remote(fsend.at[k, pl.ds(0, 7)], frecv.at[k, pl.ds(0, 7)], f_s.at[k], f_r.at[k], me).wait_send()


def solution(mesh):
    bf16 = jnp.bfloat16

    def local_step(q_blk, kv_blk, len_blk):
        q = q_blk.reshape(BATCH * 2, WIDTH)
        sets = []
        for k in range(3):
            n = COUNT[k]
            block = q[2 * BASE[k]:2 * BASE[k] + 16 * n].reshape(8, 2 * n, WIDTH)
            sets.append(jnp.pad(block, ((0, 0), (0, 16 - 2 * n), (0, 0))))
        q_sets = jnp.stack(sets)
        dma = pltpu.SemaphoreType.DMA
        out = pl.pallas_call(
            kernel,
            out_shape=jax.ShapeDtypeStruct((3, 8, 16, LATENT), bf16),
            in_specs=[
                pl.BlockSpec(memory_space=pltpu.SMEM),
                pl.BlockSpec(memory_space=pltpu.VMEM),
                pl.BlockSpec(memory_space=pl.ANY),
            ],
            out_specs=pl.BlockSpec(memory_space=pltpu.VMEM),
            scratch_shapes=[
                pltpu.VMEM((SLOTS, 8, 2, PAGE, WIDTH), bf16),
                pltpu.VMEM((3, 8, 16, WIDTH), bf16),
                pltpu.VMEM((3, 3, 16, 16, WIDTH), bf16),
                pltpu.VMEM((3, 3, 16, 16, LATENT), bf16),
                pltpu.VMEM((3, 3, 16, 16, LATENT), bf16),
                pltpu.VMEM((3, 16, 16, 128), bf16),
                pltpu.VMEM((3, 16, 16, 128), bf16),
                pltpu.VMEM((3, 8, 16, LATENT), bf16),
                pltpu.VMEM((3, 8, 16, LATENT), bf16),
                dma((SLOTS,)), dma((SLOTS,)), dma((SLOTS,)),
                dma((3,)), dma((3,)),
                dma((3,)), dma((3,)),
                dma((3,)), dma((3,)),
                dma((SLOTS,)), dma((SLOTS,)),
                dma((3,)), dma((3,)),
                dma((3,)), dma((3,)),
            ],
            compiler_params=pltpu.CompilerParams(collective_id=0, has_side_effects=True, vmem_limit_bytes=56 * 1024 * 1024),
            name='mla',
        )(len_blk, q_sets, kv_blk)
        parts = [out[k, :, :2 * COUNT[k]].reshape(8 * COUNT[k], 2, 1, LATENT) for k in range(3)]
        return jnp.concatenate(parts, axis=0)

    return jax.shard_map(local_step, mesh=mesh, in_specs=(P('dp', None, 'dcp', None), P('dp', None, 'dcp', None, None), P('dp')), out_specs=P('dp', None, 'dcp', None), check_vma=False)
```

time: 469 us -> 97.7 us (0.21)
  the two profiles are of different devices: /device:TPU:11 before, /device:TPU:1 now
where the time goes in v1:
time: 97.7 us; the launch traced here: 97.3 us
  Pallas kernels  91.8 us (94%)
  local copies, waits for them, and re-layouts  3.82 us (4%)
  other arithmetic  1.7 us (2%)
    pallas_call x1, Pallas kernels, local_step(): pl.pallas_call(kernel, out_shape=jax.ShapeDtypeStruct((3, 8, 16, LATENT),...  91.8 us

profile of v1, /device:TPU:1, one launch (start us, length us, event | category | flops | bytes accessed | tf_op | source)
XLA Modules:
  0.0 97.3 jit_solution(18018159691078282427)
XLA Ops:
  0.0 0.8 slice.23
  0.9 0.9 fusion.1
  1.8 0.1 reshape.16
  1.9 0.1 reshape.17
  2.0 0.9 pad_maximum_fusion.q_ref
  2.8 91.8 %mla.1 = bf16[3,8,16,512]{3,2,1,0:T(8,128)(2,1)} custom-call(s32[64]{0:T(128)} %len_ref.1, bf16[3,8,16,576]{3,2,1,0:T(8,128)(2,1)} %pad_maximum_fusion.q_ref, bf16[64,2,1,64,576]{4,3,2,1,0:T(8,128)(2,1)} %kv_ref.1), custom_call_target="tpu_custom_call" | custom-call | tf_op jit(solution)/shard_map/mla/pallas_call | solution.py:247
  94.6 0.9 slice.26
  95.5 0.9 fusion
  96.5 0.8 maximum_bitcast_fusion
  (6 shorter events, 0.2 us)

commit v2 on v0

v2 whole, which is shorter than its diff:
```python
import jax
import jax.numpy as jnp
from jax import lax
from jax.experimental import pallas as pl
from jax.experimental.pallas import tpu as pltpu
from jax.sharding import PartitionSpec as P

LATENT = 512
ROPE = 64
NOPE = 128
WIDTH = LATENT + ROPE
QW = LATENT + 2 * ROPE
PAGE = 64
GROUP = 128
BATCH = 64
MASKED = -1e30
SCALE = (NOPE + ROPE) ** -0.5
MESH = pl.DeviceIdType.MESH
BF16 = jnp.bfloat16
F32 = jnp.float32

SZ, SY, SX = 32, 8, 2
RING = (SZ, SY, SX)
BIG = (SX, SZ, SY)
SMALL = (SY, SX, SZ)
LAST_BIG = (True, False, True)
COUNT = (3, 3, 2)
BASE = (0, 24, 48)
SLOTS = 8


def pick(k, vals):
    return jnp.where(k == 0, vals[0], jnp.where(k == 1, vals[1], vals[2]))


def coord(me, stride):
    return lax.rem(lax.div(me, stride), 4)


def shifted(me, stride, d):
    c = coord(me, stride)
    return me + (lax.rem(c + d, 4) - c) * stride


def remote(src, dst, ssem, rsem, dev):
    return pltpu.make_async_remote_copy(src_ref=src, dst_ref=dst, send_sem=ssem, recv_sem=rsem, device_id={'dcp': dev}, device_id_type=MESH)


def split3(v):
    hi = v.astype(BF16).astype(F32)
    mid = (v - hi).astype(BF16).astype(F32)
    return hi, mid, v - hi - mid


def put_lse(old, lse, i):
    lane = lax.broadcasted_iota(jnp.int32, old.shape, len(old.shape) - 1)
    hi, mid, lo = split3(lse)
    return jnp.where(lane == i, hi, jnp.where(lane == 8 + i, mid, jnp.where(lane == 16 + i, lo, old)))


def get_lse(x, i):
    return x[..., i:i + 1] + x[..., 8 + i:9 + i] + x[..., 16 + i:17 + i]


def onehot(shape, fn):
    row = lax.broadcasted_iota(jnp.int32, shape, 0)
    col = lax.broadcasted_iota(jnp.int32, shape, 1)
    return jnp.where(fn(row, col), 1.0, 0.0).astype(BF16)


def by_set(rows, cols):
    mats = []
    for k in range(3):
        n = COUNT[k]
        mats.append(lambda r, c, k=k, n=n: (r < (k + 1) * 64) & (r >= k * 64) & ((r & 7) < 2 * n)
                    & (c == 2 * BASE[k] + ((r - k * 64) >> 3) * 2 * n + (r & 7)))
    return mats[0](rows, cols) | mats[1](rows, cols) | mats[2](rows, cols)


def kernel(len_ref, q_ref, kv_ref, out_ref, kvlocal, ropes, kvbuf, kvrope, qsend, q0buf, qbuf, obuf, r1buf, m1buf, r2buf,
           l1send, l1recv, l2send, l2recv, fsend, frecv,
           loc_s, kv_s, kv_r, kv_l, kr_s, kr_r, q0_s, q0_r, q1_s, q1_r, q2_s, q2_r, q3_s, q3_r, r1_s, r1_r, r2_s, r2_r,
           l1_s, l1_r, l2_s, l2_r, f_s, f_r):
    me = lax.axis_index('dcp')
    core = lax.rem(me, 2)
    local = pltpu.make_async_copy(kv_ref.at[:, :, 0], kvlocal, loc_s)
    local.start()

    bar = pltpu.get_barrier_semaphore()
    peers = [me + 1 - 2 * core]
    for s in (SZ, SY, SX):
        for d in (1, 2, 3):
            t = shifted(me, s, d)
            peers += [t, t + 1 - 2 * core]
    for t in peers:
        pl.semaphore_signal(bar, inc=1, device_id={'dcp': t}, device_id_type=MESH)

    perm = onehot((192, 128), by_set)
    rows = jnp.dot(perm, q_ref[...], preferred_element_type=F32).astype(BF16)
    qsend[:, :, :, pl.ds(0, LATENT)] = rows[:, :LATENT].reshape(3, 8, 8, LATENT)
    rope2 = jnp.concatenate([rows[:, LATENT:], rows[:, LATENT:]], axis=1)
    qsend[:, :, :, pl.ds(LATENT, 2 * ROPE)] = rope2.reshape(3, 8, 8, 2 * ROPE)
    l1send[...] = jnp.zeros_like(l1send)
    l2send[...] = jnp.zeros_like(l2send)
    pl.semaphore_wait(bar, len(peers))

    own = [coord(me, RING[k]) * 2 + core for k in range(3)]

    def ring_dest(k, d, flip):
        dev = shifted(me, RING[k], d)
        dcore = core
        if flip:
            dev = dev + 1 - 2 * core
            dcore = 1 - core
        return dev, coord(dev, RING[k]) * 2 + dcore

    others = [(1, 0), (3, 0), (2, 0), (1, 1), (3, 1), (2, 1), (0, 1)]

    for k in range(3):
        for d, flip in others:
            dev, o = ring_dest(k, d, flip)
            remote(qsend.at[k, o], q0buf.at[k, own[k]], q0_s.at[k], q0_r.at[k], dev).start()
        q0buf[k, own[k]] = qsend[k, own[k]]

    def latent(b):
        return kv_ref.at[b, :, 0, :, pl.ds(0, LATENT)]

    def send_cache(t, which):
        k, i = t % 3, t // 3
        for d, flip in which:
            dev, o = ring_dest(k, d, flip)
            remote(latent(BASE[k] + o * COUNT[k] + i), kvbuf.at[t, own[k]], kv_s.at[t], kv_r.at[t], dev).start()

    for t in range(3):
        send_cache(t, [(1, 0), (3, 0)])

    big = [coord(me, BIG[k]) for k in range(3)]
    small = [coord(me, SMALL[k]) for k in range(3)]
    for k in range(3):
        n = COUNT[k]
        remote(qsend.at[k, pl.ds(0, 7)], q0buf.at[k, pl.ds(0, 7)], q0_s.at[k], q0_r.at[k], me).wait_recv()
        order = onehot((n * 16, 64), lambda r, c: c == (((r & 15) >> 1) << 3) + ((r >> 4) << 1) + (r & 1))
        piece = jnp.dot(order, q0buf[k].reshape(64, QW), preferred_element_type=F32).astype(BF16)
        qbuf[k, pl.ds(0, n), big[k], small[k]] = piece.reshape(n, 16, QW)
        view = qbuf.at[k, pl.ds(0, n), big[k], small[k]]
        for d in (1, 3, 2):
            dev = shifted(me, SMALL[k] if LAST_BIG[k] else BIG[k], d)
            remote(view, view, q1_s.at[k], q1_r.at[k], dev).start()

    for t in range(3):
        send_cache(t, [(1, 1), (3, 1)])

    def block(k, idx, lo, cnt):
        n = COUNT[k]
        if LAST_BIG[k]:
            return qbuf.at[k, pl.ds(0, n), idx, pl.ds(lo, cnt)]
        return qbuf.at[k, pl.ds(0, n), pl.ds(lo, cnt), idx]

    mid = [big[k] if LAST_BIG[k] else small[k] for k in range(3)]
    axis = [BIG[k] if LAST_BIG[k] else SMALL[k] for k in range(3)]
    for k in range(3):
        three = block(k, 0, 0, 3)
        remote(three, three, q1_s.at[k], q1_r.at[k], me).wait_recv()
        view = block(k, mid[k], 0, 4)
        for j, d in enumerate((1, 3)):
            remote(view, view, q2_s.at[k, j], q2_r.at[k, j], shifted(me, axis[k], d)).start()

    local.wait()

    def pack(b, carry):
        ropes[b] = jnp.concatenate([kvlocal[b, 0, :, pl.ds(LATENT, ROPE)], kvlocal[b, 1, :, pl.ds(LATENT, ROPE)]], axis=1)
        return carry

    lax.fori_loop(0, BATCH, pack, 0, unroll=4)
    for k in range(3):
        n = COUNT[k]
        for d, flip in others:
            dev, o = ring_dest(k, d, flip)
            remote(ropes.at[pl.ds(BASE[k] + o * n, n)], kvrope.at[k, own[k], pl.ds(0, n)], kr_s.at[k], kr_r.at[k], dev).start()
        kvrope[k, own[k], pl.ds(0, n)] = ropes[pl.ds(BASE[k] + own[k] * n, n)]

    for t in range(3):
        send_cache(t, [(2, 0), (2, 1), (0, 1)])
    for t in range(SLOTS):
        k, i = t % 3, t // 3
        pltpu.make_async_copy(latent(BASE[k] + own[k] * COUNT[k] + i), kvbuf.at[t, own[k]], kv_l.at[t]).start()

    for k in range(3):
        for j, d in enumerate((1, 3)):
            whole = block(k, mid[k], 0, 4)
            remote(whole, whole, q2_s.at[k, j], q2_r.at[k, j], me).wait_recv()
            half = block(k, lax.rem(mid[k] + (3 if j == 0 else 1), 4), 2 * j, 2)
            remote(half, half, q3_s.at[k, j], q3_r.at[k, j], shifted(me, axis[k], d)).start()

    for t in range(3, SLOTS):
        send_cache(t, others)

    for k in range(3):
        n = COUNT[k]
        for j in range(2):
            half = block(k, mid[k], 0, 2)
            remote(half, half, q3_s.at[k, j], q3_r.at[k, j], me).wait_recv()
        seven = kvrope.at[k, pl.ds(0, 7), pl.ds(0, n)]
        remote(seven, seven, kr_s.at[k], kr_r.at[k], me).wait_recv()

    def attend(t, carry):
        k = lax.rem(t, 3)
        i = lax.div(t, 3)
        ring = pick(k, RING)
        u = coord(me, ring)
        bstride = pick(k, BIG)
        b_me = coord(me, bstride)
        length = len_ref[24 * k + (u * 2 + core) * pick(k, COUNT) + i]
        pltpu.make_async_copy(latent(0), kvbuf.at[t, 0], kv_l.at[t]).wait()
        seven = kvbuf.at[t, pl.ds(0, 7)]
        remote(seven, seven, kv_s.at[t], kv_r.at[t], me).wait_recv()
        q = qbuf[k, i].reshape(256, QW)
        keys = kvbuf[t].reshape(1024, LATENT)
        packed = kvrope[k, :, i]
        lane = lax.broadcasted_iota(jnp.int32, packed.shape, 2)
        zero = jnp.zeros_like(packed)
        rope = jnp.stack([jnp.where(lane < ROPE, packed, zero), jnp.where(lane >= ROPE, packed, zero)], axis=1).reshape(1024, 2 * ROPE)
        nt = (((1,), (1,)), ((), ()))
        s = lax.dot_general(q[:, :LATENT], keys, nt, preferred_element_type=F32)
        s = s + lax.dot_general(q[:, LATENT:], rope, nt, preferred_element_type=F32)
        s = s * SCALE
        kk = lax.broadcasted_iota(jnp.int32, (1, 1024), 1)
        dsrc = (me - u * ring - core) + (kk >> 8) * ring + ((kk >> 7) & 1)
        pos = (((kk >> 6) & 1) * GROUP + dsrc) * PAGE + (kk & 63)
        tok = lax.broadcasted_iota(jnp.int32, (256, 1), 0) & 1
        s = jnp.where(pos - tok <= length - 2, s, MASKED)
        m = jnp.max(s, axis=1, keepdims=True)
        w = jnp.exp(s - m)
        l = jnp.sum(w, axis=1, keepdims=True)
        part = jnp.dot(w.astype(BF16), keys, preferred_element_type=F32)
        obuf[k, i] = (part * (1.0 / l)).astype(BF16).reshape(4, 4, 16, LATENT)
        old = l1send[k].reshape(256, 128).astype(F32)
        l1send[k] = put_lse(old, m + jnp.log(l), i).astype(BF16).reshape(4, 4, 16, 128)
        for d in (1, 3, 2):
            b = lax.rem(b_me + d, 4)
            remote(obuf.at[k, i, b], r1buf.at[k, i, b_me], r1_s.at[t], r1_r.at[t], me + (b - b_me) * bstride).start()
        r1buf[k, i, b_me] = obuf[k, i, b_me]

        @pl.when(t >= 5)
        def _():
            for d in (1, 3, 2):
                b = lax.rem(b_me + d, 4)
                remote(l1send.at[k, b], l1recv.at[k, b_me], l1_s.at[k], l1_r.at[k], me + (b - b_me) * bstride).start()
            l1recv[k, b_me] = l1send[k, b_me]

        return carry

    lax.fori_loop(0, SLOTS, attend, 0)

    def merge(lse, ref):
        top = jnp.max(lse, axis=0)
        e = jnp.exp(lse - top[None])
        total = jnp.sum(e, axis=0)
        wgt = e / total[None]
        acc = wgt[0] * ref[0].astype(F32)
        for p in range(1, 4):
            acc = acc + wgt[p] * ref[p].astype(F32)
        return acc.astype(BF16), top + jnp.log(total)

    for k in (2, 0, 1):
        n = COUNT[k]
        three = l1recv.at[k, pl.ds(0, 3)]
        remote(three, three, l1_s.at[k], l1_r.at[k], me).wait_recv()
        lr = l1recv[k].astype(F32)
        lacc = jnp.zeros((4, 16, 128), F32)
        for i in range(n):
            t = 3 * i + k
            three = r1buf.at[k, i, pl.ds(0, 3)]
            remote(three, three, r1_s.at[t], r1_r.at[t], me).wait_recv()
            both, lse = merge(get_lse(lr, i), r1buf.at[k, i])
            m1buf[k, i] = both
            lacc = put_lse(lacc, lse, i)
            for d in (1, 3, 2):
                b = lax.rem(small[k] + d, 4)
                remote(m1buf.at[k, i, b], r2buf.at[k, i, small[k]], r2_s.at[t], r2_r.at[t], shifted(me, SMALL[k], d)).start()
            r2buf[k, i, small[k]] = m1buf[k, i, small[k]]
        l2send[k] = lacc.astype(BF16)
        for d in (1, 3, 2):
            b = lax.rem(small[k] + d, 4)
            remote(l2send.at[k, b], l2recv.at[k, small[k]], l2_s.at[k], l2_r.at[k], shifted(me, SMALL[k], d)).start()
        l2recv[k, small[k]] = l2send[k, small[k]]

    for k in (2, 0, 1):
        n = COUNT[k]
        three = l2recv.at[k, pl.ds(0, 3)]
        remote(three, three, l2_s.at[k], l2_r.at[k], me).wait_recv()
        lr = l2recv[k].astype(F32)
        merged = []
        for i in range(n):
            t = 3 * i + k
            three = r2buf.at[k, i, pl.ds(0, 3)]
            remote(three, three, r2_s.at[t], r2_r.at[t], me).wait_recv()
            merged.append(merge(get_lse(lr, i), r2buf.at[k, i])[0])
        order = onehot((64, n * 16), lambda r, c: r == (((c & 15) >> 1) << 3) + ((c >> 4) << 1) + (c & 1))
        out = jnp.dot(order, jnp.concatenate(merged, axis=0), preferred_element_type=F32)
        fsend[k] = out.astype(BF16).reshape(8, 8, LATENT)
        for d, flip in others:
            dev, o = ring_dest(k, d, flip)
            remote(fsend.at[k, o], frecv.at[k, own[k]], f_s.at[k], f_r.at[k], dev).start()
        frecv[k, own[k]] = fsend[k, own[k]]

    back = onehot((128, 192), lambda r, c: by_set(c, r))
    for k in range(3):
        seven = frecv.at[k, pl.ds(0, 7)]
        remote(seven, seven, f_s.at[k], f_r.at[k], me).wait_recv()
    out_ref[...] = jnp.dot(back, frecv[...].reshape(192, LATENT), preferred_element_type=F32).astype(BF16)

    def sent(view, sem):
        remote(view, view, sem, sem, me).wait_send()

    for t in range(SLOTS):
        k, i = t % 3, t // 3
        sent(kvbuf.at[t, pl.ds(0, 7)], kv_s.at[t])
        sent(r1buf.at[k, i, pl.ds(0, 3)], r1_s.at[t])
        sent(r2buf.at[k, i, pl.ds(0, 3)], r2_s.at[t])
    for k in range(3):
        n = COUNT[k]
        sent(q0buf.at[k, pl.ds(0, 7)], q0_s.at[k])
        sent(block(k, 0, 0, 3), q1_s.at[k])
        for j in range(2):
            sent(block(k, 0, 0, 4), q2_s.at[k, j])
            sent(block(k, 0, 0, 2), q3_s.at[k, j])
        sent(kvrope.at[k, pl.ds(0, 7), pl.ds(0, n)], kr_s.at[k])
        sent(l1recv.at[k, pl.ds(0, 3)], l1_s.at[k])
        sent(l2recv.at[k, pl.ds(0, 3)], l2_s.at[k])
        sent(frecv.at[k, pl.ds(0, 7)], f_s.at[k])


def solution(mesh):
    def local_step(q_blk, kv_blk, len_blk):
        dma = pltpu.SemaphoreType.DMA
        vmem = pltpu.VMEM
        out = pl.pallas_call(
            kernel,
            out_shape=jax.ShapeDtypeStruct((2 * BATCH, LATENT), BF16),
            in_specs=[
                pl.BlockSpec(memory_space=pltpu.SMEM),
                pl.BlockSpec(memory_space=pltpu.VMEM),
                pl.BlockSpec(memory_space=pl.ANY),
            ],
            out_specs=pl.BlockSpec(memory_space=pltpu.VMEM),
            scratch_shapes=[
                vmem((BATCH, 2, PAGE, WIDTH), BF16),
                vmem((BATCH, PAGE, 2 * ROPE), BF16),
                vmem((SLOTS, 8, 2, PAGE, LATENT), BF16),
                vmem((3, 8, 3, PAGE, 2 * ROPE), BF16),
                vmem((3, 8, 8, QW), BF16),
                vmem((3, 8, 8, QW), BF16),
                vmem((3, 3, 4, 4, 16, QW), BF16),
                vmem((3, 3, 4, 4, 16, LATENT), BF16),
                vmem((3, 3, 4, 4, 16, LATENT), BF16),
                vmem((3, 3, 4, 16, LATENT), BF16),
                vmem((3, 3, 4, 16, LATENT), BF16),
                vmem((3, 4, 4, 16, 128), BF16),
                vmem((3, 4, 4, 16, 128), BF16),
                vmem((3, 4, 16, 128), BF16),
                vmem((3, 4, 16, 128), BF16),
                vmem((3, 8, 8, LATENT), BF16),
                vmem((3, 8, 8, LATENT), BF16),
                dma,
                dma((SLOTS,)), dma((SLOTS,)), dma((SLOTS,)),
                dma((3,)), dma((3,)),
                dma((3,)), dma((3,)),
                dma((3,)), dma((3,)),
                dma((3, 2)), dma((3, 2)),
                dma((3, 2)), dma((3, 2)),
                dma((SLOTS,)), dma((SLOTS,)),
                dma((SLOTS,)), dma((SLOTS,)),
                dma((3,)), dma((3,)),
                dma((3,)), dma((3,)),
                dma((3,)), dma((3,)),
            ],
            compiler_params=pltpu.CompilerParams(collective_id=0, has_side_effects=True, vmem_limit_bytes=60 * 1024 * 1024),
            name='mla',
        )(len_blk, q_blk.reshape(2 * BATCH, WIDTH), kv_blk)
        return out.reshape(BATCH, 2, 1, LATENT)

    return jax.shard_map(local_step, mesh=mesh, in_specs=(P('dp', None, 'dcp', None), P('dp', None, 'dcp', None, None), P('dp')), out_specs=P('dp', None, 'dcp', None), check_vma=False)
```

time: 469 us -> 82 us (0.17)
  the two profiles are of different devices: /device:TPU:11 before, /device:TPU:1 now
where the time goes in v2:
time: 82 us; the launch traced here: 81.8 us
  Pallas kernels  78.5 us (96%)
  local copies, waits for them, and re-layouts  3.31 us (4%)
    pallas_call x1, Pallas kernels, local_step(): pl.pallas_call(kernel, out_shape=jax.ShapeDtypeStruct((2 * BATCH, LATENT)...  78.5 us
    reshape x1, local copies, waits for them, and re-layouts, local_step(): q_blk.reshape(2 * BATCH, WIDTH)  1.69 us

profile of v2, /device:TPU:1, one launch (start us, length us, event | category | flops | bytes accessed | tf_op | source)
XLA Modules:
  0.0 81.8 jit_solution(16522483455242909518)
XLA Ops:
  0.0 1.7 %reshape.6.q_ref = bf16[128,576]{1,0:T(8,128)(2,1)} reshape(bf16[64,2,1,576]{3,1,2,0:T(2,128)(2,1)} %param.3) | data formatting | bytes 294912 | tf_op jit(solution)/shard_map/reshape | solution.py:380
  1.7 78.5 %mla.1 = bf16[128,512]{1,0:T(8,128)(2,1)} custom-call(s32[64]{0:T(128)} %len_ref.1, bf16[128,576]{1,0:T(8,128)(2,1)} %reshape.6.q_ref, bf16[64,2,1,64,576]{4,3,2,1,0:T(8,128)(2,1)} %kv_ref.1), custom_call_target="tpu_custom_call" | custom-call | tf_op jit(solution)/shard_map/mla/pallas_call | solution.py:338
  80.2 1.6 %reshape.7 = bf16[64,2,1,512]{3,1,0,2:T(2,128)(2,1)} reshape(bf16[128,512]{1,0:T(8,128)(2,1)} %mla.1) | data formatting | bytes 262144 | tf_op jit(solution)/shard_map/reshape | solution.py:381

commit v3 on v2

--- a/solution.py
+++ b/solution.py
@@ -77,12 +77,14 @@
     return mats[0](rows, cols) | mats[1](rows, cols) | mats[2](rows, cols)
 
 
-def kernel(len_ref, q_ref, kv_ref, out_ref, kvlocal, ropes, kvbuf, kvrope, qsend, q0buf, qbuf, obuf, r1buf, m1buf, r2buf,
+def kernel(len_ref, q_ref, kv_ref, out_ref, qlocal, kvlocal, ropes, kvbuf, kvrope, qsend, q0buf, qbuf, obuf, r1buf, m1buf, r2buf,
            l1send, l1recv, l2send, l2recv, fsend, frecv,
-           loc_s, kv_s, kv_r, kv_l, kr_s, kr_r, q0_s, q0_r, q1_s, q1_r, q2_s, q2_r, q3_s, q3_r, r1_s, r1_r, r2_s, r2_r,
+           ql_s, loc_s, kv_s, kv_r, kv_l, kr_s, kr_r, q0_s, q0_r, q1_s, q1_r, q2_s, q2_r, q3_s, q3_r, r1_s, r1_r, r2_s, r2_r,
            l1_s, l1_r, l2_s, l2_r, f_s, f_r):
     me = lax.axis_index('dcp')
     core = lax.rem(me, 2)
+    queries = pltpu.make_async_copy(q_ref, qlocal, ql_s)
+    queries.start()
     local = pltpu.make_async_copy(kv_ref.at[:, :, 0], kvlocal, loc_s)
     local.start()
 
@@ -94,16 +96,15 @@
             peers += [t, t + 1 - 2 * core]
     for t in peers:
         pl.semaphore_signal(bar, inc=1, device_id={'dcp': t}, device_id_type=MESH)
-
     perm = onehot((192, 128), by_set)
-    rows = jnp.dot(perm, q_ref[...], preferred_element_type=F32).astype(BF16)
+    queries.wait()
+    rows = jnp.dot(perm, qlocal[...].reshape(2 * BATCH, WIDTH), preferred_element_type=F32).astype(BF16)
     qsend[:, :, :, pl.ds(0, LATENT)] = rows[:, :LATENT].reshape(3, 8, 8, LATENT)
     rope2 = jnp.concatenate([rows[:, LATENT:], rows[:, LATENT:]], axis=1)
     qsend[:, :, :, pl.ds(LATENT, 2 * ROPE)] = rope2.reshape(3, 8, 8, 2 * ROPE)
     l1send[...] = jnp.zeros_like(l1send)
     l2send[...] = jnp.zeros_like(l2send)
     pl.semaphore_wait(bar, len(peers))
-
     own = [coord(me, RING[k]) * 2 + core for k in range(3)]
 
     def ring_dest(k, d, flip):
@@ -130,10 +131,9 @@
         for d, flip in which:
             dev, o = ring_dest(k, d, flip)
             remote(latent(BASE[k] + o * COUNT[k] + i), kvbuf.at[t, own[k]], kv_s.at[t], kv_r.at[t], dev).start()
-
     for t in range(3):
-        send_cache(t, [(1, 0), (3, 0)])
-
+        send_cache(t, others[:2] + others[3:5])
+    send_cache(2, [(2, 0), (2, 1), (0, 1)])
     big = [coord(me, BIG[k]) for k in range(3)]
     small = [coord(me, SMALL[k]) for k in range(3)]
     for k in range(3):
@@ -146,16 +146,14 @@
         for d in (1, 3, 2):
             dev = shifted(me, SMALL[k] if LAST_BIG[k] else BIG[k], d)
             remote(view, view, q1_s.at[k], q1_r.at[k], dev).start()
-
-    for t in range(3):
-        send_cache(t, [(1, 1), (3, 1)])
+    for t in range(2):
+        send_cache(t, [(2, 0), (2, 1), (0, 1)])
 
     def block(k, idx, lo, cnt):
         n = COUNT[k]
         if LAST_BIG[k]:
             return qbuf.at[k, pl.ds(0, n), idx, pl.ds(lo, cnt)]
         return qbuf.at[k, pl.ds(0, n), pl.ds(lo, cnt), idx]
-
     mid = [big[k] if LAST_BIG[k] else small[k] for k in range(3)]
     axis = [BIG[k] if LAST_BIG[k] else SMALL[k] for k in range(3)]
     for k in range(3):
@@ -164,9 +162,7 @@
         view = block(k, mid[k], 0, 4)
         for j, d in enumerate((1, 3)):
             remote(view, view, q2_s.at[k, j], q2_r.at[k, j], shifted(me, axis[k], d)).start()
-
     local.wait()
-
     def pack(b, carry):
         ropes[b] = jnp.concatenate([kvlocal[b, 0, :, pl.ds(LATENT, ROPE)], kvlocal[b, 1, :, pl.ds(LATENT, ROPE)]], axis=1)
         return carry
@@ -179,22 +175,26 @@
             remote(ropes.at[pl.ds(BASE[k] + o * n, n)], kvrope.at[k, own[k], pl.ds(0, n)], kr_s.at[k], kr_r.at[k], dev).start()
         kvrope[k, own[k], pl.ds(0, n)] = ropes[pl.ds(BASE[k] + own[k] * n, n)]
 
-    for t in range(3):
-        send_cache(t, [(2, 0), (2, 1), (0, 1)])
-    for t in range(SLOTS):
-        k, i = t % 3, t // 3
-        pltpu.make_async_copy(latent(BASE[k] + own[k] * COUNT[k] + i), kvbuf.at[t, own[k]], kv_l.at[t]).start()
-
-    for k in range(3):
+    send_cache(3, others)
+    send_cache(4, others[:2])
+    send_cache(5, others[:2])
+
+    def forward(k):
         for j, d in enumerate((1, 3)):
             whole = block(k, mid[k], 0, 4)
             remote(whole, whole, q2_s.at[k, j], q2_r.at[k, j], me).wait_recv()
             half = block(k, lax.rem(mid[k] + (3 if j == 0 else 1), 4), 2 * j, 2)
             remote(half, half, q3_s.at[k, j], q3_r.at[k, j], shifted(me, axis[k], d)).start()
-
-    for t in range(3, SLOTS):
-        send_cache(t, others)
-
+    forward(2)
+    send_cache(4, others[2:])
+    send_cache(6, others)
+    send_cache(7, others)
+    forward(0)
+    forward(1)
+    send_cache(5, others[2:])
+    for t in range(SLOTS):
+        k, i = t % 3, t // 3
+        pltpu.make_async_copy(latent(BASE[k] + own[k] * COUNT[k] + i), kvbuf.at[t, own[k]], kv_l.at[t]).start()
     for k in range(3):
         n = COUNT[k]
         for j in range(2):
@@ -202,7 +202,6 @@
             remote(half, half, q3_s.at[k, j], q3_r.at[k, j], me).wait_recv()
         seven = kvrope.at[k, pl.ds(0, 7), pl.ds(0, n)]
         remote(seven, seven, kr_s.at[k], kr_r.at[k], me).wait_recv()
-
     def attend(t, carry):
         k = lax.rem(t, 3)
         i = lax.div(t, 3)
@@ -247,7 +246,6 @@
                 b = lax.rem(b_me + d, 4)
                 remote(l1send.at[k, b], l1recv.at[k, b_me], l1_s.at[k], l1_r.at[k], me + (b - b_me) * bstride).start()
             l1recv[k, b_me] = l1send[k, b_me]
-
         return carry
 
     lax.fori_loop(0, SLOTS, attend, 0)
@@ -303,13 +301,12 @@
             dev, o = ring_dest(k, d, flip)
             remote(fsend.at[k, o], frecv.at[k, own[k]], f_s.at[k], f_r.at[k], dev).start()
         frecv[k, own[k]] = fsend[k, own[k]]
-
     back = onehot((128, 192), lambda r, c: by_set(c, r))
     for k in range(3):
         seven = frecv.at[k, pl.ds(0, 7)]
         remote(seven, seven, f_s.at[k], f_r.at[k], me).wait_recv()
-    out_ref[...] = jnp.dot(back, frecv[...].reshape(192, LATENT), preferred_element_type=F32).astype(BF16)
-
+    out = jnp.dot(back, frecv[...].reshape(192, LATENT), preferred_element_type=F32)
+    out_ref[...] = out.astype(BF16).reshape(BATCH, 2, LATENT)
     def sent(view, sem):
         remote(view, view, sem, sem, me).wait_send()
 
@@ -337,14 +334,15 @@
         vmem = pltpu.VMEM
         out = pl.pallas_call(
             kernel,
-            out_shape=jax.ShapeDtypeStruct((2 * BATCH, LATENT), BF16),
+            out_shape=jax.ShapeDtypeStruct((BATCH, 2, LATENT), BF16),
             in_specs=[
                 pl.BlockSpec(memory_space=pltpu.SMEM),
-                pl.BlockSpec(memory_space=pltpu.VMEM),
-                pl.BlockSpec(memory_space=pl.ANY),
+                pl.BlockSpec(memory_space=pltpu.HBM),
+                pl.BlockSpec(memory_space=pltpu.HBM),
             ],
             out_specs=pl.BlockSpec(memory_space=pltpu.VMEM),
             scratch_shapes=[
+                vmem((BATCH, 2, WIDTH), BF16),
                 vmem((BATCH, 2, PAGE, WIDTH), BF16),
                 vmem((BATCH, PAGE, 2 * ROPE), BF16),
                 vmem((SLOTS, 8, 2, PAGE, LATENT), BF16),
@@ -362,7 +360,7 @@
                 vmem((3, 4, 16, 128), BF16),
                 vmem((3, 8, 8, LATENT), BF16),
                 vmem((3, 8, 8, LATENT), BF16),
-                dma,
+                dma, dma,
                 dma((SLOTS,)), dma((SLOTS,)), dma((SLOTS,)),
                 dma((3,)), dma((3,)),
                 dma((3,)), dma((3,)),
@@ -375,9 +373,9 @@
                 dma((3,)), dma((3,)),
                 dma((3,)), dma((3,)),
             ],
-            compiler_params=pltpu.CompilerParams(collective_id=0, has_side_effects=True, vmem_limit_bytes=60 * 1024 * 1024),
+            compiler_params=pltpu.CompilerParams(collective_id=0, has_side_effects=True, vmem_limit_bytes=44 * 1024 * 1024),
             name='mla',
-        )(len_blk, q_blk.reshape(2 * BATCH, WIDTH), kv_blk)
+        )(len_blk, q_blk.reshape(BATCH, 2, WIDTH), kv_blk)
         return out.reshape(BATCH, 2, 1, LATENT)
 
     return jax.shard_map(local_step, mesh=mesh, in_specs=(P('dp', None, 'dcp', None), P('dp', None, 'dcp', None, None), P('dp')), out_specs=P('dp', None, 'dcp', None), check_vma=False)

time: 82 us -> 78.5 us (0.957)
  Pallas kernels: 78.5 us -> 76.1 us
  local copies, waits for them, and re-layouts: 3.31 us -> 2.23 us
    reshape x2 -> x0, local copies, waits for them, and re-layouts: 3.31 us -> none  [the longest x1 1.69 us: local_step(): q_blk.reshape(2 * BATCH, WIDTH)]
    pallas_call x1, Pallas kernels: 78.5 us -> 76.1 us  [local_step(): pl.pallas_call(kernel, out_shape=jax.ShapeDtypeStruct((BATCH, 2, LATENT),...]
    unnamed x0 -> x5, local copies, waits for them, and re-layouts: none -> 2.23 us
where the time goes in v3:
time: 78.5 us; the launch traced here: 78.4 us
  Pallas kernels  76.1 us (97%)
  local copies, waits for them, and re-layouts  2.23 us (3%)
    pallas_call x1, Pallas kernels, local_step(): pl.pallas_call(kernel, out_shape=jax.ShapeDtypeStruct((BATCH, 2, LATENT),...  76.1 us
    unnamed x5, local copies, waits for them, and re-layouts  2.23 us

profile of v3, /device:TPU:1, one launch (start us, length us, event | category | flops | bytes accessed | tf_op | source)
XLA Modules:
  0.0 78.4 jit_solution(17623034025822146409)
XLA Ops:
  0.0 0.0 copy-start
  0.0 0.9 %copy-done = bf16[64,2,1,576]{3,1,2,0:T(2,128)(2,1)S(1)} copy-done((bf16[64,2,1,576]{3,1,2,0:T(2,128)(2,1)S(1)}, bf16[64,2,1,576]{3,1,2,0:T(2,128)(2,1)}, u32[]{:S(2)}) %copy-start) | copy-done | bytes 147480
  0.9 0.0 copy-start.1
  0.9 0.7 copy-done.1
  1.6 76.1 %mla.1 = bf16[64,2,512]{2,1,0:T(2,128)(2,1)S(1)} custom-call(s32[64]{0:T(128)S(1)} %copy-done.1, bf16[64,2,576]{2,1,0:T(2,128)(2,1)S(1)} %bitcast.5, bf16[64,2,1,64,576]{4,3,2,1,0:T(8,128)(2,1)} %kv_ref.1), custom_call_target="tpu_custom_call" | custom-call | tf_op jit(solution)/shard_map/mla/pallas_call | solution.py:335
  77.7 0.7 copy.6
Async XLA Ops:
  0.0 0.9 %copy-start = (bf16[64,2,1,576]{3,1,2,0:T(2,128)(2,1)S(1)}, bf16[64,2,1,576]{3,1,2,0:T(2,128)(2,1)}, u32[]{:S(2)}) copy-start(bf16[64,2,1,576]{3,1,2,0:T(2,128)(2,1)} %param.3) | copy-start | bytes 442372
  0.9 0.7 copy-start.1

commit v4 on v3

--- a/solution.py
+++ b/solution.py
@@ -58,6 +58,19 @@
     return jnp.where(lane == i, hi, jnp.where(lane == 8 + i, mid, jnp.where(lane == 16 + i, lo, old)))
 
 
+def tile_lse(lse):
+    tile = jnp.zeros((4, 16, 128), F32)
+    lane = lax.broadcasted_iota(jnp.int32, tile.shape, 2)
+    for b in range(4):
+        for j, v in enumerate(split3(lse[:, b])):
+            tile = jnp.where(lane == 32 * b + j, v, tile)
+    return tile.astype(BF16)
+
+
+def untile_lse(x):
+    return jnp.stack([x[..., 32 * b:32 * b + 1] + x[..., 32 * b + 1:32 * b + 2] + x[..., 32 * b + 2:32 * b + 3] for b in range(4)], axis=1)
+
+
 def get_lse(x, i):
     return x[..., i:i + 1] + x[..., 8 + i:9 + i] + x[..., 16 + i:17 + i]
 
@@ -77,14 +90,16 @@
     return mats[0](rows, cols) | mats[1](rows, cols) | mats[2](rows, cols)
 
 
-def kernel(len_ref, q_ref, kv_ref, out_ref, qlocal, kvlocal, ropes, kvbuf, kvrope, qsend, q0buf, qbuf, obuf, r1buf, m1buf, r2buf,
+def kernel(len_hbm, q_ref, kv_ref, out_ref, len_ref, qlocal, kvlocal, ropes, kvbuf, kvrope, qsend, q0buf, qbuf, obuf, r1buf, m1buf, r2buf,
            l1send, l1recv, l2send, l2recv, fsend, frecv,
-           ql_s, loc_s, kv_s, kv_r, kv_l, kr_s, kr_r, q0_s, q0_r, q1_s, q1_r, q2_s, q2_r, q3_s, q3_r, r1_s, r1_r, r2_s, r2_r,
+           len_s, ql_s, loc_s, kv_s, kv_r, kv_l, kr_s, kr_r, q0_s, q0_r, q1_s, q1_r, q2_s, q2_r, q3_s, q3_r, r1_s, r1_r, r2_s, r2_r,
            l1_s, l1_r, l2_s, l2_r, f_s, f_r):
     me = lax.axis_index('dcp')
     core = lax.rem(me, 2)
     queries = pltpu.make_async_copy(q_ref, qlocal, ql_s)
     queries.start()
+    lens = pltpu.make_async_copy(len_hbm, len_ref, len_s)
+    lens.start()
     local = pltpu.make_async_copy(kv_ref.at[:, :, 0], kvlocal, loc_s)
     local.start()
 
@@ -102,8 +117,6 @@
     qsend[:, :, :, pl.ds(0, LATENT)] = rows[:, :LATENT].reshape(3, 8, 8, LATENT)
     rope2 = jnp.concatenate([rows[:, LATENT:], rows[:, LATENT:]], axis=1)
     qsend[:, :, :, pl.ds(LATENT, 2 * ROPE)] = rope2.reshape(3, 8, 8, 2 * ROPE)
-    l1send[...] = jnp.zeros_like(l1send)
-    l2send[...] = jnp.zeros_like(l2send)
     pl.semaphore_wait(bar, len(peers))
     own = [coord(me, RING[k]) * 2 + core for k in range(3)]
 
@@ -195,6 +208,8 @@
     for t in range(SLOTS):
         k, i = t % 3, t // 3
         pltpu.make_async_copy(latent(BASE[k] + own[k] * COUNT[k] + i), kvbuf.at[t, own[k]], kv_l.at[t]).start()
+
+    lens.wait()
     for k in range(3):
         n = COUNT[k]
         for j in range(2):
@@ -233,19 +248,13 @@
         l = jnp.sum(w, axis=1, keepdims=True)
         part = jnp.dot(w.astype(BF16), keys, preferred_element_type=F32)
         obuf[k, i] = (part * (1.0 / l)).astype(BF16).reshape(4, 4, 16, LATENT)
-        old = l1send[k].reshape(256, 128).astype(F32)
-        l1send[k] = put_lse(old, m + jnp.log(l), i).astype(BF16).reshape(4, 4, 16, 128)
+        l1send[k, i] = tile_lse((m + jnp.log(l)).reshape(4, 4, 16, 1))
         for d in (1, 3, 2):
             b = lax.rem(b_me + d, 4)
             remote(obuf.at[k, i, b], r1buf.at[k, i, b_me], r1_s.at[t], r1_r.at[t], me + (b - b_me) * bstride).start()
+            remote(l1send.at[k, i, b], l1recv.at[k, i, b_me], l1_s.at[t], l1_r.at[t], me + (b - b_me) * bstride).start()
         r1buf[k, i, b_me] = obuf[k, i, b_me]
-
-        @pl.when(t >= 5)
-        def _():
-            for d in (1, 3, 2):
-                b = lax.rem(b_me + d, 4)
-                remote(l1send.at[k, b], l1recv.at[k, b_me], l1_s.at[k], l1_r.at[k], me + (b - b_me) * bstride).start()
-            l1recv[k, b_me] = l1send[k, b_me]
+        l1recv[k, i, b_me] = l1send[k, i, b_me]
         return carry
 
     lax.fori_loop(0, SLOTS, attend, 0)
@@ -260,28 +269,26 @@
             acc = acc + wgt[p] * ref[p].astype(F32)
         return acc.astype(BF16), top + jnp.log(total)
 
-    for k in (2, 0, 1):
-        n = COUNT[k]
-        three = l1recv.at[k, pl.ds(0, 3)]
-        remote(three, three, l1_s.at[k], l1_r.at[k], me).wait_recv()
-        lr = l1recv[k].astype(F32)
-        lacc = jnp.zeros((4, 16, 128), F32)
-        for i in range(n):
-            t = 3 * i + k
-            three = r1buf.at[k, i, pl.ds(0, 3)]
-            remote(three, three, r1_s.at[t], r1_r.at[t], me).wait_recv()
-            both, lse = merge(get_lse(lr, i), r1buf.at[k, i])
-            m1buf[k, i] = both
-            lacc = put_lse(lacc, lse, i)
+    lacc = [jnp.zeros((4, 16, 128), F32) for _ in range(3)]
+    for t in (0, 2, 1, 3, 5, 4, 6, 7):
+        k, i = t % 3, t // 3
+        three = l1recv.at[k, i, pl.ds(0, 3)]
+        remote(three, three, l1_s.at[t], l1_r.at[t], me).wait_recv()
+        three = r1buf.at[k, i, pl.ds(0, 3)]
+        remote(three, three, r1_s.at[t], r1_r.at[t], me).wait_recv()
+        both, lse = merge(untile_lse(l1recv[k, i].astype(F32)), r1buf.at[k, i])
+        m1buf[k, i] = both
+        lacc[k] = put_lse(lacc[k], lse, i)
+        for d in (1, 3, 2):
+            b = lax.rem(small[k] + d, 4)
+            remote(m1buf.at[k, i, b], r2buf.at[k, i, small[k]], r2_s.at[t], r2_r.at[t], shifted(me, SMALL[k], d)).start()
+        r2buf[k, i, small[k]] = m1buf[k, i, small[k]]
+        if i == COUNT[k] - 1:
+            l2send[k] = lacc[k].astype(BF16)
             for d in (1, 3, 2):
                 b = lax.rem(small[k] + d, 4)
-                remote(m1buf.at[k, i, b], r2buf.at[k, i, small[k]], r2_s.at[t], r2_r.at[t], shifted(me, SMALL[k], d)).start()
-            r2buf[k, i, small[k]] = m1buf[k, i, small[k]]
-        l2send[k] = lacc.astype(BF16)
-        for d in (1, 3, 2):
-            b = lax.rem(small[k] + d, 4)
-            remote(l2send.at[k, b], l2recv.at[k, small[k]], l2_s.at[k], l2_r.at[k], shifted(me, SMALL[k], d)).start()
-        l2recv[k, small[k]] = l2send[k, small[k]]
+                remote(l2send.at[k, b], l2recv.at[k, small[k]], l2_s.at[k], l2_r.at[k], shifted(me, SMALL[k], d)).start()
+            l2recv[k, small[k]] = l2send[k, small[k]]
 
     for k in (2, 0, 1):
         n = COUNT[k]
@@ -315,6 +322,7 @@
         sent(kvbuf.at[t, pl.ds(0, 7)], kv_s.at[t])
         sent(r1buf.at[k, i, pl.ds(0, 3)], r1_s.at[t])
         sent(r2buf.at[k, i, pl.ds(0, 3)], r2_s.at[t])
+        sent(l1recv.at[k, i, pl.ds(0, 3)], l1_s.at[t])
     for k in range(3):
         n = COUNT[k]
         sent(q0buf.at[k, pl.ds(0, 7)], q0_s.at[k])
@@ -323,7 +331,6 @@
             sent(block(k, 0, 0, 4), q2_s.at[k, j])
             sent(block(k, 0, 0, 2), q3_s.at[k, j])
         sent(kvrope.at[k, pl.ds(0, 7), pl.ds(0, n)], kr_s.at[k])
-        sent(l1recv.at[k, pl.ds(0, 3)], l1_s.at[k])
         sent(l2recv.at[k, pl.ds(0, 3)], l2_s.at[k])
         sent(frecv.at[k, pl.ds(0, 7)], f_s.at[k])
 
@@ -332,16 +339,21 @@
     def local_step(q_blk, kv_blk, len_blk):
         dma = pltpu.SemaphoreType.DMA
         vmem = pltpu.VMEM
+
+        def hbm(v):
+            return pltpu.with_memory_space_constraint(v, pltpu.HBM)
+
         out = pl.pallas_call(
             kernel,
             out_shape=jax.ShapeDtypeStruct((BATCH, 2, LATENT), BF16),
             in_specs=[
-                pl.BlockSpec(memory_space=pltpu.SMEM),
+                pl.BlockSpec(memory_space=pltpu.HBM),
                 pl.BlockSpec(memory_space=pltpu.HBM),
                 pl.BlockSpec(memory_space=pltpu.HBM),
             ],
             out_specs=pl.BlockSpec(memory_space=pltpu.VMEM),
             scratch_shapes=[
+                pltpu.SMEM((BATCH,), jnp.int32),
                 vmem((BATCH, 2, WIDTH), BF16),
                 vmem((BATCH, 2, PAGE, WIDTH), BF16),
                 vmem((BATCH, PAGE, 2 * ROPE), BF16),
@@ -354,13 +366,13 @@
                 vmem((3, 3, 4, 4, 16, LATENT), BF16),
                 vmem((3, 3, 4, 16, LATENT), BF16),
                 vmem((3, 3, 4, 16, LATENT), BF16),
-                vmem((3, 4, 4, 16, 128), BF16),
-                vmem((3, 4, 4, 16, 128), BF16),
+                vmem((3, 3, 4, 16, 128), BF16),
+                vmem((3, 3, 4, 16, 128), BF16),
                 vmem((3, 4, 16, 128), BF16),
                 vmem((3, 4, 16, 128), BF16),
                 vmem((3, 8, 8, LATENT), BF16),
                 vmem((3, 8, 8, LATENT), BF16),
-                dma, dma,
+                dma, dma, dma,
                 dma((SLOTS,)), dma((SLOTS,)), dma((SLOTS,)),
                 dma((3,)), dma((3,)),
                 dma((3,)), dma((3,)),
@@ -369,13 +381,13 @@
                 dma((3, 2)), dma((3, 2)),
                 dma((SLOTS,)), dma((SLOTS,)),
                 dma((SLOTS,)), dma((SLOTS,)),
-                dma((3,)), dma((3,)),
+                dma((SLOTS,)), dma((SLOTS,)),
                 dma((3,)), dma((3,)),
                 dma((3,)), dma((3,)),
             ],
             compiler_params=pltpu.CompilerParams(collective_id=0, has_side_effects=True, vmem_limit_bytes=44 * 1024 * 1024),
             name='mla',
-        )(len_blk, q_blk.reshape(BATCH, 2, WIDTH), kv_blk)
+        )(hbm(len_blk), hbm(q_blk.reshape(BATCH, 2, WIDTH)), kv_blk)
         return out.reshape(BATCH, 2, 1, LATENT)
 
     return jax.shard_map(local_step, mesh=mesh, in_specs=(P('dp', None, 'dcp', None), P('dp', None, 'dcp', None, None), P('dp')), out_specs=P('dp', None, 'dcp', None), check_vma=False)

time: 78.5 us -> 76 us (0.968)
  local copies, waits for them, and re-layouts: 2.23 us -> 0.66 us
  Pallas kernels: 76.1 us -> 75.2 us
    unnamed x5 -> x1, local copies, waits for them, and re-layouts: 2.23 us -> 0.66 us
    pallas_call x1, Pallas kernels: 76.1 us -> 75.2 us  [local_step(): pl.pallas_call(kernel, out_shape=jax.ShapeDtypeStruct((BATCH, 2, LATENT),...]
where the time goes in v4:
time: 76 us; the launch traced here: 75.9 us
  Pallas kernels  75.2 us (99%)
    pallas_call x1, Pallas kernels, local_step(): pl.pallas_call(kernel, out_shape=jax.ShapeDtypeStruct((BATCH, 2, LATENT),...  75.2 us

profile of v4, /device:TPU:1, one launch (start us, length us, event | category | flops | bytes accessed | tf_op | source)
XLA Modules:
  0.0 75.9 jit_solution(13296063188822869626)
XLA Ops:
  0.0 75.2 %mla.1 = bf16[64,2,512]{2,1,0:T(2,128)(2,1)S(1)} custom-call(s32[64]{0:T(128)} %len_hbm.1, bf16[64,2,576]{2,1,0:T(2,128)(2,1)} %bitcast.5, bf16[64,2,1,64,576]{4,3,2,1,0:T(8,128)(2,1)} %kv_ref.1), custom_call_target="tpu_custom_call" | custom-call | tf_op jit(solution)/shard_map/mla/pallas_call | solution.py:346
  75.2 0.7 copy.6

commit v5 on v4

v5 whole, which is shorter than its diff:
```python
import jax
import jax.numpy as jnp
from jax import lax
from jax.experimental import pallas as pl
from jax.experimental.pallas import tpu as pltpu
from jax.sharding import PartitionSpec as P

LATENT = 512
ROPE = 64
NOPE = 128
WIDTH = LATENT + ROPE
QW = 2 * LATENT + 2 * ROPE
PAGE = 64
GROUP = 128
BATCH = 64
MASKED = -1e30
SCALE = (NOPE + ROPE) ** -0.5
MESH = pl.DeviceIdType.MESH
BF16 = jnp.bfloat16
F32 = jnp.float32

SZ, SY, SX = 32, 8, 2
RING = (SZ, SY, SX)
BIG = (SX, SZ, SY)
SMALL = (SY, SX, SZ)
COUNT = (3, 3, 2)
BASE = (0, 24, 48)
SLOTS = 8
LATE = 7
UNITS = ((0, 0, 3, True), (1, 0, 3, False), (2, 0, 1, True), (2, 1, 1, False))


def pick(k, vals):
    return jnp.where(k == 0, vals[0], jnp.where(k == 1, vals[1], vals[2]))


def coord(me, stride):
    return lax.rem(lax.div(me, stride), 4)


def shifted(me, stride, d):
    c = coord(me, stride)
    return me + (lax.rem(c + d, 4) - c) * stride


def remote(src, dst, ssem, rsem, dev):
    return pltpu.make_async_remote_copy(src_ref=src, dst_ref=dst, send_sem=ssem, recv_sem=rsem, device_id={'dcp': dev}, device_id_type=MESH)


def arrived(view, sem):
    pltpu.make_async_copy(view, view, sem).wait()


def split3(v):
    hi = v.astype(BF16).astype(F32)
    mid = (v - hi).astype(BF16).astype(F32)
    return hi, mid, v - hi - mid


def put_lse(old, lse, i):
    lane = lax.broadcasted_iota(jnp.int32, old.shape, len(old.shape) - 1)
    hi, mid, lo = split3(lse)
    return jnp.where(lane == i, hi, jnp.where(lane == 8 + i, mid, jnp.where(lane == 16 + i, lo, old)))


def tile_lse(lse):
    tile = jnp.zeros((4, 16, 128), F32)
    lane = lax.broadcasted_iota(jnp.int32, tile.shape, 2)
    for b in range(4):
        for j, v in enumerate(split3(lse[:, b])):
            tile = jnp.where(lane == 32 * b + j, v, tile)
    return tile.astype(BF16)


def untile_lse(x):
    return jnp.stack([x[..., 32 * b:32 * b + 1] + x[..., 32 * b + 1:32 * b + 2] + x[..., 32 * b + 2:32 * b + 3] for b in range(4)], axis=1)


def get_lse(x, i):
    return x[..., i:i + 1] + x[..., 8 + i:9 + i] + x[..., 16 + i:17 + i]


def onehot(shape, fn):
    row = lax.broadcasted_iota(jnp.int32, shape, 0)
    col = lax.broadcasted_iota(jnp.int32, shape, 1)
    return jnp.where(fn(row, col), 1.0, 0.0).astype(BF16)


def by_set(rows, cols, pad, tokens, tok):
    hit = None
    for k in range(3):
        n = COUNT[k]
        r = rows - k * 8 * pad
        o, j = lax.div(jnp.maximum(r, 0), pad), r & (pad - 1)
        m = (r >= 0) & (r < 8 * pad) & (j < n * tokens) & (cols == 2 * (BASE[k] + o * n) + (2 // tokens) * j + tok)
        hit = m if hit is None else hit | m
    return hit


def kernel(len_hbm, q_ref, kv_ref, out_ref, len_ref, qlocal, kvlocal, ropes, kvbuf, kvrope, qsend, q0buf, qbuf, obuf, r1buf, m1buf, r2buf,
           l1send, l1recv, l2send, l2recv, dbuf, dlse, fsend, frecv,
           len_s, ql_s, loc_s, kv_s, kv_r, kv_l, kr_s, kr_r, q0_s, q0_r, q1_s, q1_r, q2_s, q2_r, q3_s, q3_r, r1_s, r1_r, r2_s, r2_r,
           l1_s, l1_r, l2_s, l2_r, d_s, d_r, dl_s, dl_r, f_s, f_r):
    me = lax.axis_index('dcp')
    core = lax.rem(me, 2)
    queries = pltpu.make_async_copy(q_ref, qlocal, ql_s)
    queries.start()
    lens = pltpu.make_async_copy(len_hbm, len_ref, len_s)
    lens.start()
    local = pltpu.make_async_copy(kv_ref.at[:, :, 0], kvlocal, loc_s)
    local.start()

    bar = pltpu.get_barrier_semaphore()
    peers = [me + 1 - 2 * core]
    for s in (SZ, SY, SX):
        for d in (1, 2, 3):
            t = shifted(me, s, d)
            peers += [t, t + 1 - 2 * core]
    for d1 in (1, 2, 3):
        for d2 in (1, 2, 3):
            peers.append(shifted(shifted(me, BIG[1], d1), SMALL[1], d2))
    for t in peers:
        pl.semaphore_signal(bar, inc=1, device_id={'dcp': t}, device_id_type=MESH)
    perms = [onehot((96, 128), lambda r, c, tok=tok: by_set(r, c, 4, 1, tok)) for tok in range(2)]
    queries.wait()
    both = [jnp.dot(perm, qlocal[...].reshape(2 * BATCH, WIDTH), preferred_element_type=F32).astype(BF16) for perm in perms]
    for tok in range(2):
        qsend[:, :, :, pl.ds(tok * LATENT, LATENT)] = both[tok][:, :LATENT].reshape(3, 8, 4, LATENT)
    rotary = jnp.concatenate([both[0][:, LATENT:], both[1][:, LATENT:]], axis=1)
    qsend[:, :, :, pl.ds(2 * LATENT, 2 * ROPE)] = rotary.reshape(3, 8, 4, 2 * ROPE)
    pl.semaphore_wait(bar, len(peers))
    own = [coord(me, RING[k]) * 2 + core for k in range(3)]

    def ring_dest(k, d, flip):
        dev = shifted(me, RING[k], d)
        dcore = core
        if flip:
            dev = dev + 1 - 2 * core
            dcore = 1 - core
        return dev, coord(dev, RING[k]) * 2 + dcore

    others = [(1, 0), (3, 0), (2, 0), (1, 1), (3, 1), (2, 1), (0, 1)]

    for k in range(3):
        for d, flip in others:
            dev, o = ring_dest(k, d, flip)
            remote(qsend.at[k, o], q0buf.at[k, own[k]], q0_s, q0_r, dev).start()
        q0buf[k, own[k]] = qsend[k, own[k]]

    def latent(b):
        return kv_ref.at[b, :, 0, :, pl.ds(0, LATENT)]

    def send_cache(t, which):
        k, i = t % 3, t // 3
        for d, flip in which:
            dev, o = ring_dest(k, d, flip)
            remote(latent(BASE[k] + o * COUNT[k] + i), kvbuf.at[t, own[k]], kv_s, kv_r.at[t], dev).start()
    for t in range(3):
        send_cache(t, others[:2] + others[3:5])
    send_cache(2, [(2, 0), (2, 1), (0, 1)])
    big = [coord(me, BIG[k]) for k in range(3)]
    small = [coord(me, SMALL[k]) for k in range(3)]
    arrived(q0buf.at[:, pl.ds(0, 7)], q0_r)
    for k in range(3):
        n = COUNT[k]
        order = onehot((n * 8, 32), lambda r, c: c == ((r & 7) << 2) + (r >> 3))
        piece = jnp.dot(order, q0buf[k].reshape(32, QW), preferred_element_type=F32).astype(BF16)
        qbuf[k, pl.ds(0, n), big[k], small[k]] = piece.reshape(n, 8, QW)
    for j, (k, i, n, last_big) in enumerate(UNITS):
        view = qbuf.at[k, pl.ds(i, n), big[k], small[k]]
        for d in (1, 3, 2):
            dev = shifted(me, SMALL[k] if last_big else BIG[k], d)
            remote(view, view, q1_s, q1_r.at[j], dev).start()
    for t in range(2):
        send_cache(t, [(2, 0), (2, 1), (0, 1)])

    def block(u, idx, lo, cnt):
        k, i, n, last_big = UNITS[u]
        if last_big:
            return qbuf.at[k, pl.ds(i, n), idx, pl.ds(lo, cnt)]
        return qbuf.at[k, pl.ds(i, n), pl.ds(lo, cnt), idx]

    mid = [big[k] if last_big else small[k] for k, i, n, last_big in UNITS]
    axis = [BIG[k] if last_big else SMALL[k] for k, i, n, last_big in UNITS]
    for u in range(4):
        arrived(block(u, 0, 0, 3), q1_r.at[u])
        view = block(u, mid[u], 0, 4)
        for j, d in enumerate((1, 3)):
            remote(view, view, q2_s, q2_r.at[u, j], shifted(me, axis[u], d)).start()
    local.wait()
    def pack(b, carry):
        ropes[b] = jnp.concatenate([kvlocal[b, 0, :, pl.ds(LATENT, ROPE)], kvlocal[b, 1, :, pl.ds(LATENT, ROPE)]], axis=1)
        return carry

    lax.fori_loop(0, BATCH, pack, 0, unroll=4)
    for k in range(3):
        n = COUNT[k]
        for d, flip in others:
            dev, o = ring_dest(k, d, flip)
            remote(ropes.at[pl.ds(BASE[k] + o * n, n)], kvrope.at[k, own[k], pl.ds(0, n)], kr_s, kr_r, dev).start()
        kvrope[k, own[k], pl.ds(0, n)] = ropes[pl.ds(BASE[k] + own[k] * n, n)]

    send_cache(3, others)
    send_cache(4, others[:2])
    send_cache(5, others[:2])

    def forward(k):
        for j, d in enumerate((1, 3)):
            arrived(block(k, mid[k], 0, 4), q2_r.at[k, j])
            half = block(k, lax.rem(mid[k] + (3 if j == 0 else 1), 4), 2 * j, 2)
            remote(half, half, q3_s, q3_r, shifted(me, axis[k], d)).start()
    forward(2)
    forward(3)
    send_cache(4, others[2:])
    send_cache(6, others)
    send_cache(7, others)
    forward(0)
    forward(1)
    send_cache(5, others[2:])
    for t in range(SLOTS):
        k, i = t % 3, t // 3
        pltpu.make_async_copy(latent(BASE[k] + own[k] * COUNT[k] + i), kvbuf.at[t, own[k]], kv_l).start()

    lens.wait()
    arrived(qbuf.at[pl.ds(0, 2), 0], q3_r)
    arrived(ropes.at[pl.ds(0, 56)], kr_r)
    arrived(kvbuf.at[:, 0], kv_l)
    def attend(t, carry):
        k = lax.rem(t, 3)
        i = lax.div(t, 3)
        ring = pick(k, RING)
        u = coord(me, ring)
        bstride = pick(k, BIG)
        b_me = coord(me, bstride)
        length = len_ref[24 * k + (u * 2 + core) * pick(k, COUNT) + i]
        arrived(kvbuf.at[t, pl.ds(0, 7)], kv_r.at[t])
        q2 = qbuf[k, i].reshape(128, QW)
        q = jnp.concatenate([q2[:, :LATENT], q2[:, LATENT:2 * LATENT]], axis=0)
        pair = q2[:, 2 * LATENT:]
        swapped = jnp.concatenate([pair[:, ROPE:], pair[:, :ROPE]], axis=1)
        low = lax.broadcasted_iota(jnp.int32, pair.shape, 1) < ROPE
        qr = jnp.concatenate([jnp.where(low, pair, swapped), jnp.where(low, swapped, pair)], axis=0)
        keys = kvbuf[t].reshape(1024, LATENT)
        packed = kvrope[k, :, i]
        lane = lax.broadcasted_iota(jnp.int32, packed.shape, 2)
        zero = jnp.zeros_like(packed)
        rope = jnp.stack([jnp.where(lane < ROPE, packed, zero), jnp.where(lane >= ROPE, packed, zero)], axis=1).reshape(1024, 2 * ROPE)
        nt = (((1,), (1,)), ((), ()))
        s = lax.dot_general(q, keys, nt, preferred_element_type=F32)
        s = s + lax.dot_general(qr, rope, nt, preferred_element_type=F32)
        s = s * SCALE
        kk = lax.broadcasted_iota(jnp.int32, (1, 1024), 1)
        dsrc = (me - u * ring - core) + (kk >> 8) * ring + ((kk >> 7) & 1)
        pos = (((kk >> 6) & 1) * GROUP + dsrc) * PAGE + (kk & 63)
        tok = lax.broadcasted_iota(jnp.int32, (256, 1), 0) >> 7
        s = jnp.where(pos - tok <= length - 2, s, MASKED)
        m = jnp.max(s, axis=1, keepdims=True)
        w = jnp.exp(s - m)
        l = jnp.sum(w, axis=1, keepdims=True)
        part = jnp.dot(w.astype(BF16), keys, preferred_element_type=F32)
        part = (part * (1.0 / l)).astype(BF16)
        obuf[k, i, :, :, pl.ds(0, 8)] = part[:128].reshape(4, 4, 8, LATENT)
        obuf[k, i, :, :, pl.ds(8, 8)] = part[128:].reshape(4, 4, 8, LATENT)
        lse = m + jnp.log(l)
        l1send[k, i] = tile_lse(jnp.concatenate([lse[:128].reshape(4, 4, 8, 1), lse[128:].reshape(4, 4, 8, 1)], axis=2))

        @pl.when(t < LATE)
        def _():
            for d in (1, 3, 2):
                b = lax.rem(b_me + d, 4)
                dev = me + (b - b_me) * bstride
                remote(obuf.at[k, i, b], r1buf.at[t, b_me], r1_s, r1_r.at[t], dev).start()
                remote(l1send.at[k, i, b], l1recv.at[t, b_me], l1_s, l1_r.at[t], dev).start()
            r1buf[t, b_me] = obuf[k, i, b_me]
            l1recv[t, b_me] = l1send[k, i, b_me]

        @pl.when(t == LATE)
        def _():
            place = big[1] * 4 + small[1]
            for d1, d2 in ((1, 0), (3, 0), (0, 1), (0, 3), (1, 1), (1, 3), (3, 1), (3, 3), (2, 0), (0, 2), (1, 2), (3, 2), (2, 1), (2, 3), (2, 2)):
                b1, b2 = lax.rem(big[1] + d1, 4), lax.rem(small[1] + d2, 4)
                dev = me + (b1 - big[1]) * BIG[1] + (b2 - small[1]) * SMALL[1]
                remote(obuf.at[1, 2, b1, b2], dbuf.at[place], d_s, d_r, dev).start()
                remote(l1send.at[1, 2, b1], dlse.at[place], dl_s, dl_r, dev).start()
            dbuf[place] = obuf[1, 2, big[1], small[1]]
            dlse[place] = l1send[1, 2, big[1]]
        return carry

    lax.fori_loop(0, SLOTS, attend, 0)

    def merge(lse, ref):
        top = jnp.max(lse, axis=0)
        e = jnp.exp(lse - top[None])
        total = jnp.sum(e, axis=0)
        wgt = e / total[None]
        acc = wgt[0] * ref[0].astype(F32)
        for p in range(1, ref.shape[0]):
            acc = acc + wgt[p] * ref[p].astype(F32)
        return acc.astype(BF16), top + jnp.log(total)

    lacc = [jnp.zeros((4, 16, 128), F32) for _ in range(3)]
    for t in (0, 2, 1, 3, 5, 4, 6):
        k, i = t % 3, t // 3
        arrived(l1recv.at[t, pl.ds(0, 3)], l1_r.at[t])
        arrived(r1buf.at[t, pl.ds(0, 3)], r1_r.at[t])
        both, lse = merge(untile_lse(l1recv[t].astype(F32)), r1buf.at[t])
        m1buf[k, i] = both
        lacc[k] = put_lse(lacc[k], lse, i)
        for d in (1, 3, 2):
            b = lax.rem(small[k] + d, 4)
            remote(m1buf.at[k, i, b], r2buf.at[t, small[k]], r2_s, r2_r.at[k], shifted(me, SMALL[k], d)).start()
        r2buf[t, small[k]] = m1buf[k, i, small[k]]
        if t >= 4:
            l2send[k] = lacc[k].astype(BF16)
            for d in (1, 3, 2):
                b = lax.rem(small[k] + d, 4)
                remote(l2send.at[k, b], l2recv.at[k, small[k]], l2_s, l2_r.at[k], shifted(me, SMALL[k], d)).start()
            l2recv[k, small[k]] = l2send[k, small[k]]

    for k in (2, 0, 1):
        n = COUNT[k]
        if k == LATE % 3:
            arrived(dlse.at[pl.ds(0, 15)], dl_r)
            arrived(dbuf.at[pl.ds(0, 15)], d_r)
            x = dlse[...].astype(F32)
            lse = jnp.zeros((16, 16, 1), F32)
            for b in range(4):
                v = x[..., 32 * b:32 * b + 1] + x[..., 32 * b + 1:32 * b + 2] + x[..., 32 * b + 2:32 * b + 3]
                lse = jnp.where(small[k] == b, v, lse)
            late = merge(lse, dbuf)[0]
        arrived(l2recv.at[k, pl.ds(0, 3)], l2_r.at[k])
        arrived(r2buf.at[pl.ds(0, n if k != LATE % 3 else n - 1), pl.ds(0, 3)], r2_r.at[k])
        lr = l2recv[k].astype(F32)
        merged = []
        for i in range(n):
            t = 3 * i + k
            if t == LATE:
                merged.append(late)
                continue
            merged.append(merge(get_lse(lr, i), r2buf.at[t])[0])
        order = onehot((64, n * 16), lambda r, c: r == ((c & 7) << 3) + ((c >> 4) << 1) + ((c >> 3) & 1))
        out = jnp.dot(order, jnp.concatenate(merged, axis=0), preferred_element_type=F32)
        fsend[k] = out.astype(BF16).reshape(8, 8, LATENT)
        for d, flip in others:
            dev, o = ring_dest(k, d, flip)
            remote(fsend.at[k, o], frecv.at[k, own[k]], f_s, f_r, dev).start()
        frecv[k, own[k]] = fsend[k, own[k]]
    back = onehot((128, 192), lambda r, c: by_set(c, r, 8, 2, 0))
    arrived(frecv.at[:, pl.ds(0, 7)], f_r)
    out = jnp.dot(back, frecv[...].reshape(192, LATENT), preferred_element_type=F32)
    out_ref[...] = out.astype(BF16).reshape(BATCH, 2, LATENT)
    def sent(view, sem):
        remote(view, view, sem, sem, me).wait_send()

    sent(q0buf.at[:, pl.ds(0, 7)], q0_s)
    sent(qbuf.at[pl.ds(0, 2), :, :, 0], q1_s)
    sent(qbuf.at[pl.ds(0, 2), pl.ds(0, 2)], q2_s)
    sent(qbuf.at[pl.ds(0, 2), 0], q3_s)
    sent(ropes.at[pl.ds(0, 56)], kr_s)
    sent(kvbuf.at[:, pl.ds(0, 7)], kv_s)
    sent(r1buf.at[pl.ds(0, LATE), pl.ds(0, 3)], r1_s)
    sent(l1recv.at[pl.ds(0, LATE), pl.ds(0, 3)], l1_s)
    sent(r2buf.at[pl.ds(0, LATE), pl.ds(0, 3)], r2_s)
    sent(l2recv.at[:, pl.ds(0, 3)], l2_s)
    sent(dbuf.at[pl.ds(0, 15)], d_s)
    sent(dlse.at[pl.ds(0, 15)], dl_s)
    sent(frecv.at[:, pl.ds(0, 7)], f_s)


def solution(mesh):
    def local_step(q_blk, kv_blk, len_blk):
        dma = pltpu.SemaphoreType.DMA
        vmem = pltpu.VMEM

        def hbm(v):
            return pltpu.with_memory_space_constraint(v, pltpu.HBM)

        out = pl.pallas_call(
            kernel,
            out_shape=jax.ShapeDtypeStruct((BATCH, 2, LATENT), BF16),
            in_specs=[
                pl.BlockSpec(memory_space=pltpu.HBM),
                pl.BlockSpec(memory_space=pltpu.HBM),
                pl.BlockSpec(memory_space=pltpu.HBM),
            ],
            out_specs=pl.BlockSpec(memory_space=pltpu.VMEM),
            scratch_shapes=[
                pltpu.SMEM((BATCH,), jnp.int32),
                vmem((BATCH, 2, WIDTH), BF16),
                vmem((BATCH, 2, PAGE, WIDTH), BF16),
                vmem((BATCH, PAGE, 2 * ROPE), BF16),
                vmem((SLOTS, 8, 2, PAGE, LATENT), BF16),
                vmem((3, 8, 3, PAGE, 2 * ROPE), BF16),
                vmem((3, 8, 4, QW), BF16),
                vmem((3, 8, 4, QW), BF16),
                vmem((3, 3, 4, 4, 8, QW), BF16),
                vmem((3, 3, 4, 4, 16, LATENT), BF16),
                vmem((SLOTS, 4, 4, 16, LATENT), BF16),
                vmem((3, 3, 4, 16, LATENT), BF16),
                vmem((SLOTS, 4, 16, LATENT), BF16),
                vmem((3, 3, 4, 16, 128), BF16),
                vmem((SLOTS, 4, 16, 128), BF16),
                vmem((3, 4, 16, 128), BF16),
                vmem((3, 4, 16, 128), BF16),
                vmem((16, 16, LATENT), BF16),
                vmem((16, 16, 128), BF16),
                vmem((3, 8, 8, LATENT), BF16),
                vmem((3, 8, 8, LATENT), BF16),
                dma, dma, dma,
                dma, dma((SLOTS,)), dma,
                dma, dma,
                dma, dma,
                dma, dma((4,)),
                dma, dma((4, 2)),
                dma, dma,
                dma, dma((SLOTS,)),
                dma, dma((3,)),
                dma, dma((SLOTS,)),
                dma, dma((3,)),
                dma, dma, dma, dma,
                dma, dma,
            ],
            compiler_params=pltpu.CompilerParams(collective_id=0, has_side_effects=True, vmem_limit_bytes=44 * 1024 * 1024),
            name='mla',
        )(hbm(len_blk), hbm(q_blk.reshape(BATCH, 2, WIDTH)), kv_blk)
        return out.reshape(BATCH, 2, 1, LATENT)

    return jax.shard_map(local_step, mesh=mesh, in_specs=(P('dp', None, 'dcp', None), P('dp', None, 'dcp', None, None), P('dp')), out_specs=P('dp', None, 'dcp', None), check_vma=False)
```

time: 76 us -> 73.3 us (0.964)
  Pallas kernels: 75.2 us -> 72.5 us
    pallas_call x1, Pallas kernels: 75.2 us -> 72.5 us  [local_step(): pl.pallas_call(kernel, out_shape=jax.ShapeDtypeStruct((BATCH, 2, LATENT),...]
where the time goes in v5:
time: 73.3 us; the launch traced here: 73.2 us
  Pallas kernels  72.5 us (99%)
    pallas_call x1, Pallas kernels, local_step(): pl.pallas_call(kernel, out_shape=jax.ShapeDtypeStruct((BATCH, 2, LATENT),...  72.5 us

profile of v5, /device:TPU:1, one launch (start us, length us, event | category | flops | bytes accessed | tf_op | source)
XLA Modules:
  0.0 73.2 jit_solution(11007047550648338422)
XLA Ops:
  0.0 72.5 %mla.1 = bf16[64,2,512]{2,1,0:T(2,128)(2,1)S(1)} custom-call(s32[64]{0:T(128)} %len_hbm.1, bf16[64,2,576]{2,1,0:T(2,128)(2,1)} %bitcast.5, bf16[64,2,1,64,576]{4,3,2,1,0:T(8,128)(2,1)} %kv_ref.1), custom_call_target="tpu_custom_call" | custom-call | tf_op jit(solution)/shard_map/mla/pallas_call | solution.py:378
  72.5 0.7 copy.6

commit v6 on v5

--- a/solution.py
+++ b/solution.py
@@ -26,8 +26,9 @@
 COUNT = (3, 3, 2)
 BASE = (0, 24, 48)
 SLOTS = 8
-LATE = 7
-UNITS = ((0, 0, 3, True), (1, 0, 3, False), (2, 0, 1, True), (2, 1, 1, False))
+STEPS = (1, 3, 2)
+SENDS = (2, 1, 3)
+UNITS = ((0, 0, 3, True), (1, 0, 3, False), (2, 0, 1, True), (2, 1, 1, True))
 
 
 def pick(k, vals):
@@ -57,27 +58,30 @@
     return hi, mid, v - hi - mid
 
 
-def put_lse(old, lse, i):
-    lane = lax.broadcasted_iota(jnp.int32, old.shape, len(old.shape) - 1)
-    hi, mid, lo = split3(lse)
-    return jnp.where(lane == i, hi, jnp.where(lane == 8 + i, mid, jnp.where(lane == 16 + i, lo, old)))
+def put_lse(tile, lse, b):
+    lane = lax.broadcasted_iota(jnp.int32, tile.shape, len(tile.shape) - 1)
+    for j, v in enumerate(split3(lse)):
+        tile = jnp.where(lane == 32 * b + j, v, tile)
+    return tile
+
+
+def get_lse(x, b):
+    return sum(x[..., 32 * b + j:32 * b + j + 1] for j in range(3))
 
 
 def tile_lse(lse):
     tile = jnp.zeros((4, 16, 128), F32)
-    lane = lax.broadcasted_iota(jnp.int32, tile.shape, 2)
     for b in range(4):
-        for j, v in enumerate(split3(lse[:, b])):
-            tile = jnp.where(lane == 32 * b + j, v, tile)
+        tile = put_lse(tile, lse[:, b], b)
     return tile.astype(BF16)
 
 
 def untile_lse(x):
-    return jnp.stack([x[..., 32 * b:32 * b + 1] + x[..., 32 * b + 1:32 * b + 2] + x[..., 32 * b + 2:32 * b + 3] for b in range(4)], axis=1)
-
-
-def get_lse(x, i):
-    return x[..., i:i + 1] + x[..., 8 + i:9 + i] + x[..., 16 + i:17 + i]
+    return jnp.stack([get_lse(x, b) for b in range(4)], axis=1)
+
+
+def first(count):
+    return pl.ds(0, count)
 
 
 def onehot(shape, fn):
@@ -98,9 +102,9 @@
 
 
 def kernel(len_hbm, q_ref, kv_ref, out_ref, len_ref, qlocal, kvlocal, ropes, kvbuf, kvrope, qsend, q0buf, qbuf, obuf, r1buf, m1buf, r2buf,
-           l1send, l1recv, l2send, l2recv, dbuf, dlse, fsend, frecv,
+           l1send, l1recv, l2send, l2recv, fsend, frecv,
            len_s, ql_s, loc_s, kv_s, kv_r, kv_l, kr_s, kr_r, q0_s, q0_r, q1_s, q1_r, q2_s, q2_r, q3_s, q3_r, r1_s, r1_r, r2_s, r2_r,
-           l1_s, l1_r, l2_s, l2_r, d_s, d_r, dl_s, dl_r, f_s, f_r):
+           l1_s, l1_r, l2_s, l2_r, f_s, f_r):
     me = lax.axis_index('dcp')
     core = lax.rem(me, 2)
     queries = pltpu.make_async_copy(q_ref, qlocal, ql_s)
@@ -113,12 +117,9 @@
     bar = pltpu.get_barrier_semaphore()
     peers = [me + 1 - 2 * core]
     for s in (SZ, SY, SX):
-        for d in (1, 2, 3):
+        for d in STEPS:
             t = shifted(me, s, d)
             peers += [t, t + 1 - 2 * core]
-    for d1 in (1, 2, 3):
-        for d2 in (1, 2, 3):
-            peers.append(shifted(shifted(me, BIG[1], d1), SMALL[1], d2))
     for t in peers:
         pl.semaphore_signal(bar, inc=1, device_id={'dcp': t}, device_id_type=MESH)
     perms = [onehot((96, 128), lambda r, c, tok=tok: by_set(r, c, 4, 1, tok)) for tok in range(2)]
@@ -139,7 +140,9 @@
             dcore = 1 - core
         return dev, coord(dev, RING[k]) * 2 + dcore
 
-    others = [(1, 0), (3, 0), (2, 0), (1, 1), (3, 1), (2, 1), (0, 1)]
+    near = [(d, flip) for flip in range(2) for d in STEPS[:2]]
+    far = [(STEPS[2], flip) for flip in range(2)] + [(0, 1)]
+    others = near + far
 
     for k in range(3):
         for d, flip in others:
@@ -148,7 +151,7 @@
         q0buf[k, own[k]] = qsend[k, own[k]]
 
     def latent(b):
-        return kv_ref.at[b, :, 0, :, pl.ds(0, LATENT)]
+        return kv_ref.at[b, :, 0, :, first(LATENT)]
 
     def send_cache(t, which):
         k, i = t % 3, t // 3
@@ -156,23 +159,23 @@
             dev, o = ring_dest(k, d, flip)
             remote(latent(BASE[k] + o * COUNT[k] + i), kvbuf.at[t, own[k]], kv_s, kv_r.at[t], dev).start()
     for t in range(3):
-        send_cache(t, others[:2] + others[3:5])
-    send_cache(2, [(2, 0), (2, 1), (0, 1)])
+        send_cache(t, near)
+    send_cache(2, far)
     big = [coord(me, BIG[k]) for k in range(3)]
     small = [coord(me, SMALL[k]) for k in range(3)]
-    arrived(q0buf.at[:, pl.ds(0, 7)], q0_r)
+    arrived(q0buf.at[:, first(7)], q0_r)
     for k in range(3):
         n = COUNT[k]
         order = onehot((n * 8, 32), lambda r, c: c == ((r & 7) << 2) + (r >> 3))
         piece = jnp.dot(order, q0buf[k].reshape(32, QW), preferred_element_type=F32).astype(BF16)
-        qbuf[k, pl.ds(0, n), big[k], small[k]] = piece.reshape(n, 8, QW)
+        qbuf[k, first(n), big[k], small[k]] = piece.reshape(n, 8, QW)
     for j, (k, i, n, last_big) in enumerate(UNITS):
         view = qbuf.at[k, pl.ds(i, n), big[k], small[k]]
-        for d in (1, 3, 2):
+        for d in STEPS:
             dev = shifted(me, SMALL[k] if last_big else BIG[k], d)
             remote(view, view, q1_s, q1_r.at[j], dev).start()
     for t in range(2):
-        send_cache(t, [(2, 0), (2, 1), (0, 1)])
+        send_cache(t, far)
 
     def block(u, idx, lo, cnt):
         k, i, n, last_big = UNITS[u]
@@ -185,7 +188,7 @@
     for u in range(4):
         arrived(block(u, 0, 0, 3), q1_r.at[u])
         view = block(u, mid[u], 0, 4)
-        for j, d in enumerate((1, 3)):
+        for j, d in enumerate(STEPS[:2]):
             remote(view, view, q2_s, q2_r.at[u, j], shifted(me, axis[u], d)).start()
     local.wait()
     def pack(b, carry):
@@ -197,15 +200,15 @@
         n = COUNT[k]
         for d, flip in others:
             dev, o = ring_dest(k, d, flip)
-            remote(ropes.at[pl.ds(BASE[k] + o * n, n)], kvrope.at[k, own[k], pl.ds(0, n)], kr_s, kr_r, dev).start()
-        kvrope[k, own[k], pl.ds(0, n)] = ropes[pl.ds(BASE[k] + own[k] * n, n)]
+            remote(ropes.at[pl.ds(BASE[k] + o * n, n)], kvrope.at[k, own[k], first(n)], kr_s, kr_r, dev).start()
+        kvrope[k, own[k], first(n)] = ropes[pl.ds(BASE[k] + own[k] * n, n)]
 
     send_cache(3, others)
     send_cache(4, others[:2])
     send_cache(5, others[:2])
 
     def forward(k):
-        for j, d in enumerate((1, 3)):
+        for j, d in enumerate(STEPS[:2]):
             arrived(block(k, mid[k], 0, 4), q2_r.at[k, j])
             half = block(k, lax.rem(mid[k] + (3 if j == 0 else 1), 4), 2 * j, 2)
             remote(half, half, q3_s, q3_r, shifted(me, axis[k], d)).start()
@@ -222,8 +225,8 @@
         pltpu.make_async_copy(latent(BASE[k] + own[k] * COUNT[k] + i), kvbuf.at[t, own[k]], kv_l).start()
 
     lens.wait()
-    arrived(qbuf.at[pl.ds(0, 2), 0], q3_r)
-    arrived(ropes.at[pl.ds(0, 56)], kr_r)
+    arrived(qbuf.at[first(2), 0], q3_r)
+    arrived(ropes.at[first(56)], kr_r)
     arrived(kvbuf.at[:, 0], kv_l)
     def attend(t, carry):
         k = lax.rem(t, 3)
@@ -233,7 +236,7 @@
         bstride = pick(k, BIG)
         b_me = coord(me, bstride)
         length = len_ref[24 * k + (u * 2 + core) * pick(k, COUNT) + i]
-        arrived(kvbuf.at[t, pl.ds(0, 7)], kv_r.at[t])
+        arrived(kvbuf.at[t, first(7)], kv_r.at[t])
         q2 = qbuf[k, i].reshape(128, QW)
         q = jnp.concatenate([q2[:, :LATENT], q2[:, LATENT:2 * LATENT]], axis=0)
         pair = q2[:, 2 * LATENT:]
@@ -259,31 +262,17 @@
         l = jnp.sum(w, axis=1, keepdims=True)
         part = jnp.dot(w.astype(BF16), keys, preferred_element_type=F32)
         part = (part * (1.0 / l)).astype(BF16)
-        obuf[k, i, :, :, pl.ds(0, 8)] = part[:128].reshape(4, 4, 8, LATENT)
+        obuf[k, i, :, :, first(8)] = part[:128].reshape(4, 4, 8, LATENT)
         obuf[k, i, :, :, pl.ds(8, 8)] = part[128:].reshape(4, 4, 8, LATENT)
         lse = m + jnp.log(l)
         l1send[k, i] = tile_lse(jnp.concatenate([lse[:128].reshape(4, 4, 8, 1), lse[128:].reshape(4, 4, 8, 1)], axis=2))
-
-        @pl.when(t < LATE)
-        def _():
-            for d in (1, 3, 2):
-                b = lax.rem(b_me + d, 4)
-                dev = me + (b - b_me) * bstride
-                remote(obuf.at[k, i, b], r1buf.at[t, b_me], r1_s, r1_r.at[t], dev).start()
-                remote(l1send.at[k, i, b], l1recv.at[t, b_me], l1_s, l1_r.at[t], dev).start()
-            r1buf[t, b_me] = obuf[k, i, b_me]
-            l1recv[t, b_me] = l1send[k, i, b_me]
-
-        @pl.when(t == LATE)
-        def _():
-            place = big[1] * 4 + small[1]
-            for d1, d2 in ((1, 0), (3, 0), (0, 1), (0, 3), (1, 1), (1, 3), (3, 1), (3, 3), (2, 0), (0, 2), (1, 2), (3, 2), (2, 1), (2, 3), (2, 2)):
-                b1, b2 = lax.rem(big[1] + d1, 4), lax.rem(small[1] + d2, 4)
-                dev = me + (b1 - big[1]) * BIG[1] + (b2 - small[1]) * SMALL[1]
-                remote(obuf.at[1, 2, b1, b2], dbuf.at[place], d_s, d_r, dev).start()
-                remote(l1send.at[1, 2, b1], dlse.at[place], dl_s, dl_r, dev).start()
-            dbuf[place] = obuf[1, 2, big[1], small[1]]
-            dlse[place] = l1send[1, 2, big[1]]
+        for d in SENDS:
+            b = lax.rem(b_me + d, 4)
+            dev = me + (b - b_me) * bstride
+            remote(obuf.at[k, i, b], r1buf.at[t, b_me], r1_s, r1_r.at[t], dev).start()
+            remote(l1send.at[k, i, b], l1recv.at[t, b_me], l1_s, l1_r.at[t], dev).start()
+        r1buf[t, b_me] = obuf[k, i, b_me]
+        l1recv[t, b_me] = l1send[k, i, b_me]
         return carry
 
     lax.fori_loop(0, SLOTS, attend, 0)
@@ -299,72 +288,58 @@
         return acc.astype(BF16), top + jnp.log(total)
 
     lacc = [jnp.zeros((4, 16, 128), F32) for _ in range(3)]
-    for t in (0, 2, 1, 3, 5, 4, 6):
+    for t in (0, 2, 1, 3, 5, 4, 6, 7):
         k, i = t % 3, t // 3
-        arrived(l1recv.at[t, pl.ds(0, 3)], l1_r.at[t])
-        arrived(r1buf.at[t, pl.ds(0, 3)], r1_r.at[t])
+        arrived(l1recv.at[t, first(3)], l1_r.at[t])
+        arrived(r1buf.at[t, first(3)], r1_r.at[t])
         both, lse = merge(untile_lse(l1recv[t].astype(F32)), r1buf.at[t])
         m1buf[k, i] = both
         lacc[k] = put_lse(lacc[k], lse, i)
-        for d in (1, 3, 2):
+        for d in SENDS:
             b = lax.rem(small[k] + d, 4)
             remote(m1buf.at[k, i, b], r2buf.at[t, small[k]], r2_s, r2_r.at[k], shifted(me, SMALL[k], d)).start()
         r2buf[t, small[k]] = m1buf[k, i, small[k]]
-        if t >= 4:
+        if i == COUNT[k] - 1:
             l2send[k] = lacc[k].astype(BF16)
-            for d in (1, 3, 2):
+            for d in SENDS:
                 b = lax.rem(small[k] + d, 4)
                 remote(l2send.at[k, b], l2recv.at[k, small[k]], l2_s, l2_r.at[k], shifted(me, SMALL[k], d)).start()
             l2recv[k, small[k]] = l2send[k, small[k]]
 
     for k in (2, 0, 1):
         n = COUNT[k]
-        if k == LATE % 3:
-            arrived(dlse.at[pl.ds(0, 15)], dl_r)
-            arrived(dbuf.at[pl.ds(0, 15)], d_r)
-            x = dlse[...].astype(F32)
-            lse = jnp.zeros((16, 16, 1), F32)
-            for b in range(4):
-                v = x[..., 32 * b:32 * b + 1] + x[..., 32 * b + 1:32 * b + 2] + x[..., 32 * b + 2:32 * b + 3]
-                lse = jnp.where(small[k] == b, v, lse)
-            late = merge(lse, dbuf)[0]
-        arrived(l2recv.at[k, pl.ds(0, 3)], l2_r.at[k])
-        arrived(r2buf.at[pl.ds(0, n if k != LATE % 3 else n - 1), pl.ds(0, 3)], r2_r.at[k])
+        arrived(l2recv.at[k, first(3)], l2_r.at[k])
+        arrived(r2buf.at[first(n), first(3)], r2_r.at[k])
         lr = l2recv[k].astype(F32)
         merged = []
         for i in range(n):
             t = 3 * i + k
-            if t == LATE:
-                merged.append(late)
-                continue
             merged.append(merge(get_lse(lr, i), r2buf.at[t])[0])
         order = onehot((64, n * 16), lambda r, c: r == ((c & 7) << 3) + ((c >> 4) << 1) + ((c >> 3) & 1))
         out = jnp.dot(order, jnp.concatenate(merged, axis=0), preferred_element_type=F32)
         fsend[k] = out.astype(BF16).reshape(8, 8, LATENT)
-        for d, flip in others:
+        for d, flip in far + near:
             dev, o = ring_dest(k, d, flip)
             remote(fsend.at[k, o], frecv.at[k, own[k]], f_s, f_r, dev).start()
         frecv[k, own[k]] = fsend[k, own[k]]
     back = onehot((128, 192), lambda r, c: by_set(c, r, 8, 2, 0))
-    arrived(frecv.at[:, pl.ds(0, 7)], f_r)
+    arrived(frecv.at[:, first(7)], f_r)
     out = jnp.dot(back, frecv[...].reshape(192, LATENT), preferred_element_type=F32)
     out_ref[...] = out.astype(BF16).reshape(BATCH, 2, LATENT)
     def sent(view, sem):
         remote(view, view, sem, sem, me).wait_send()
 
-    sent(q0buf.at[:, pl.ds(0, 7)], q0_s)
-    sent(qbuf.at[pl.ds(0, 2), :, :, 0], q1_s)
-    sent(qbuf.at[pl.ds(0, 2), pl.ds(0, 2)], q2_s)
-    sent(qbuf.at[pl.ds(0, 2), 0], q3_s)
-    sent(ropes.at[pl.ds(0, 56)], kr_s)
-    sent(kvbuf.at[:, pl.ds(0, 7)], kv_s)
-    sent(r1buf.at[pl.ds(0, LATE), pl.ds(0, 3)], r1_s)
-    sent(l1recv.at[pl.ds(0, LATE), pl.ds(0, 3)], l1_s)
-    sent(r2buf.at[pl.ds(0, LATE), pl.ds(0, 3)], r2_s)
-    sent(l2recv.at[:, pl.ds(0, 3)], l2_s)
-    sent(dbuf.at[pl.ds(0, 15)], d_s)
-    sent(dlse.at[pl.ds(0, 15)], dl_s)
-    sent(frecv.at[:, pl.ds(0, 7)], f_s)
+    sent(q0buf.at[:, first(7)], q0_s)
+    sent(qbuf.at[first(2), :, :, 0], q1_s)
+    sent(qbuf.at[first(2), first(2)], q2_s)
+    sent(qbuf.at[first(2), 0], q3_s)
+    sent(ropes.at[first(56)], kr_s)
+    sent(kvbuf.at[:, first(7)], kv_s)
+    sent(r1buf.at[first(SLOTS), first(3)], r1_s)
+    sent(l1recv.at[first(SLOTS), first(3)], l1_s)
+    sent(r2buf.at[first(SLOTS), first(3)], r2_s)
+    sent(l2recv.at[:, first(3)], l2_s)
+    sent(frecv.at[:, first(7)], f_s)
 
 
 def solution(mesh):
@@ -402,8 +377,6 @@
                 vmem((SLOTS, 4, 16, 128), BF16),
                 vmem((3, 4, 16, 128), BF16),
                 vmem((3, 4, 16, 128), BF16),
-                vmem((16, 16, LATENT), BF16),
-                vmem((16, 16, 128), BF16),
                 vmem((3, 8, 8, LATENT), BF16),
                 vmem((3, 8, 8, LATENT), BF16),
                 dma, dma, dma,
@@ -417,7 +390,6 @@
                 dma, dma((3,)),
                 dma, dma((SLOTS,)),
                 dma, dma((3,)),
-                dma, dma, dma, dma,
                 dma, dma,
             ],
             compiler_params=pltpu.CompilerParams(collective_id=0, has_side_effects=True, vmem_limit_bytes=44 * 1024 * 1024),

time: 73.3 us -> 72.4 us (0.988)
  Pallas kernels: 72.5 us -> 71.7 us
    pallas_call x1, Pallas kernels: 72.5 us -> 71.7 us  [local_step(): pl.pallas_call(kernel, out_shape=jax.ShapeDtypeStruct((BATCH, 2, LATENT),...]
where the time goes in v6:
time: 72.4 us; the launch traced here: 72.3 us
  Pallas kernels  71.7 us (99%)
    pallas_call x1, Pallas kernels, local_step(): pl.pallas_call(kernel, out_shape=jax.ShapeDtypeStruct((BATCH, 2, LATENT),...  71.7 us

profile of v6, /device:TPU:1, one launch (start us, length us, event | category | flops | bytes accessed | tf_op | source)
XLA Modules:
  0.0 72.3 jit_solution(16136610591785499780)
XLA Ops:
  0.0 71.7 %mla.1 = bf16[64,2,512]{2,1,0:T(2,128)(2,1)S(1)} custom-call(s32[64]{0:T(128)} %len_hbm.1, bf16[64,2,576]{2,1,0:T(2,128)(2,1)} %bitcast.5, bf16[64,2,1,64,576]{4,3,2,1,0:T(8,128)(2,1)} %kv_ref.1), custom_call_target="tpu_custom_call" | custom-call | tf_op jit(solution)/shard_map/mla/pallas_call | solution.py:353
  71.7 0.7 copy.6

commit v7 on v6

--- a/solution.py
+++ b/solution.py
@@ -28,7 +28,7 @@
 SLOTS = 8
 STEPS = (1, 3, 2)
 SENDS = (2, 1, 3)
-UNITS = ((0, 0, 3, True), (1, 0, 3, False), (2, 0, 1, True), (2, 1, 1, True))
+UNITS = ((0, 0, 3, True), (1, 0, 3, False), (2, 0, 2, True))
 
 
 def pick(k, vals):
@@ -185,7 +185,7 @@
 
     mid = [big[k] if last_big else small[k] for k, i, n, last_big in UNITS]
     axis = [BIG[k] if last_big else SMALL[k] for k, i, n, last_big in UNITS]
-    for u in range(4):
+    for u in range(3):
         arrived(block(u, 0, 0, 3), q1_r.at[u])
         view = block(u, mid[u], 0, 4)
         for j, d in enumerate(STEPS[:2]):
@@ -211,9 +211,8 @@
         for j, d in enumerate(STEPS[:2]):
             arrived(block(k, mid[k], 0, 4), q2_r.at[k, j])
             half = block(k, lax.rem(mid[k] + (3 if j == 0 else 1), 4), 2 * j, 2)
-            remote(half, half, q3_s, q3_r, shifted(me, axis[k], d)).start()
+            remote(half, half, q3_s, q3_r.at[k], shifted(me, axis[k], d)).start()
     forward(2)
-    forward(3)
     send_cache(4, others[2:])
     send_cache(6, others)
     send_cache(7, others)
@@ -225,7 +224,6 @@
         pltpu.make_async_copy(latent(BASE[k] + own[k] * COUNT[k] + i), kvbuf.at[t, own[k]], kv_l).start()
 
     lens.wait()
-    arrived(qbuf.at[first(2), 0], q3_r)
     arrived(ropes.at[first(56)], kr_r)
     arrived(kvbuf.at[:, 0], kv_l)
     def attend(t, carry):
@@ -236,6 +234,11 @@
         bstride = pick(k, BIG)
         b_me = coord(me, bstride)
         length = len_ref[24 * k + (u * 2 + core) * pick(k, COUNT) + i]
+        for unit in range(3):
+
+            @pl.when(t == unit)
+            def _():
+                arrived(block(unit, 0, 0, 4), q3_r.at[unit])
         arrived(kvbuf.at[t, first(7)], kv_r.at[t])
         q2 = qbuf[k, i].reshape(128, QW)
         q = jnp.concatenate([q2[:, :LATENT], q2[:, LATENT:2 * LATENT]], axis=0)
@@ -383,9 +386,9 @@
                 dma, dma((SLOTS,)), dma,
                 dma, dma,
                 dma, dma,
-                dma, dma((4,)),
-                dma, dma((4, 2)),
-                dma, dma,
+                dma, dma((3,)),
+                dma, dma((3, 2)),
+                dma, dma((3,)),
                 dma, dma((SLOTS,)),
                 dma, dma((3,)),
                 dma, dma((SLOTS,)),

time: 72.4 us -> 72.2 us (level)
  no operation moved by 1% of the time
where the time goes in v7:
time: 72.2 us; the launch traced here: 72.1 us
  Pallas kernels  71.4 us (99%)
    pallas_call x1, Pallas kernels, local_step(): pl.pallas_call(kernel, out_shape=jax.ShapeDtypeStruct((BATCH, 2, LATENT),...  71.4 us

profile of v7, /device:TPU:1, one launch (start us, length us, event | category | flops | bytes accessed | tf_op | source)
XLA Modules:
  0.0 72.1 jit_solution(14809218742568948508)
XLA Ops:
  0.0 71.4 %mla.1 = bf16[64,2,512]{2,1,0:T(2,128)(2,1)S(1)} custom-call(s32[64]{0:T(128)} %len_hbm.1, bf16[64,2,576]{2,1,0:T(2,128)(2,1)} %bitcast.5, bf16[64,2,1,64,576]{4,3,2,1,0:T(8,128)(2,1)} %kv_ref.1), custom_call_target="tpu_custom_call" | custom-call | tf_op jit(solution)/shard_map/mla/pallas_call | solution.py:356
  71.4 0.7 copy.6

commit v8 on v7

--- a/solution.py
+++ b/solution.py
@@ -102,9 +102,9 @@
 
 
 def kernel(len_hbm, q_ref, kv_ref, out_ref, len_ref, qlocal, kvlocal, ropes, kvbuf, kvrope, qsend, q0buf, qbuf, obuf, r1buf, m1buf, r2buf,
-           l1send, l1recv, l2send, l2recv, fsend, frecv,
+           l1send, l1recv, l2send, l2recv, tally, fsend, frecv,
            len_s, ql_s, loc_s, kv_s, kv_r, kv_l, kr_s, kr_r, q0_s, q0_r, q1_s, q1_r, q2_s, q2_r, q3_s, q3_r, r1_s, r1_r, r2_s, r2_r,
-           l1_s, l1_r, l2_s, l2_r, f_s, f_r):
+           l1_s, l2_s, f_s, f_r):
     me = lax.axis_index('dcp')
     core = lax.rem(me, 2)
     queries = pltpu.make_async_copy(q_ref, qlocal, ql_s)
@@ -273,7 +273,7 @@
             b = lax.rem(b_me + d, 4)
             dev = me + (b - b_me) * bstride
             remote(obuf.at[k, i, b], r1buf.at[t, b_me], r1_s, r1_r.at[t], dev).start()
-            remote(l1send.at[k, i, b], l1recv.at[t, b_me], l1_s, l1_r.at[t], dev).start()
+            remote(l1send.at[k, i, b], l1recv.at[t, b_me], l1_s, r1_r.at[t], dev).start()
         r1buf[t, b_me] = obuf[k, i, b_me]
         l1recv[t, b_me] = l1send[k, i, b_me]
         return carry
@@ -291,10 +291,9 @@
         return acc.astype(BF16), top + jnp.log(total)
 
     lacc = [jnp.zeros((4, 16, 128), F32) for _ in range(3)]
-    for t in (0, 2, 1, 3, 5, 4, 6, 7):
+    for t in (0, 1, 3, 4, 2, 6, 5, 7):
         k, i = t % 3, t // 3
-        arrived(l1recv.at[t, first(3)], l1_r.at[t])
-        arrived(r1buf.at[t, first(3)], r1_r.at[t])
+        arrived(tally.at[first(51)], r1_r.at[t])
         both, lse = merge(untile_lse(l1recv[t].astype(F32)), r1buf.at[t])
         m1buf[k, i] = both
         lacc[k] = put_lse(lacc[k], lse, i)
@@ -306,13 +305,12 @@
             l2send[k] = lacc[k].astype(BF16)
             for d in SENDS:
                 b = lax.rem(small[k] + d, 4)
-                remote(l2send.at[k, b], l2recv.at[k, small[k]], l2_s, l2_r.at[k], shifted(me, SMALL[k], d)).start()
+                remote(l2send.at[k, b], l2recv.at[k, small[k]], l2_s, r2_r.at[k], shifted(me, SMALL[k], d)).start()
             l2recv[k, small[k]] = l2send[k, small[k]]
 
-    for k in (2, 0, 1):
+    for k in (0, 2, 1):
         n = COUNT[k]
-        arrived(l2recv.at[k, first(3)], l2_r.at[k])
-        arrived(r2buf.at[first(n), first(3)], r2_r.at[k])
+        arrived(tally.at[first(12 * n + 3)], r2_r.at[k])
         lr = l2recv[k].astype(F32)
         merged = []
         for i in range(n):
@@ -380,6 +378,7 @@
                 vmem((SLOTS, 4, 16, 128), BF16),
                 vmem((3, 4, 16, 128), BF16),
                 vmem((3, 4, 16, 128), BF16),
+                vmem((51, 16, 128), BF16),
                 vmem((3, 8, 8, LATENT), BF16),
                 vmem((3, 8, 8, LATENT), BF16),
                 dma, dma, dma,
@@ -391,8 +390,7 @@
                 dma, dma((3,)),
                 dma, dma((SLOTS,)),
                 dma, dma((3,)),
-                dma, dma((SLOTS,)),
-                dma, dma((3,)),
+                dma, dma,
                 dma, dma,
             ],
             compiler_params=pltpu.CompilerParams(collective_id=0, has_side_effects=True, vmem_limit_bytes=44 * 1024 * 1024),

time: 72.2 us -> 72.1 us (level)
  no operation moved by 1% of the time
where the time goes in v8:
time: 72.1 us; the launch traced here: 72 us
  Pallas kernels  71.3 us (99%)
    pallas_call x1, Pallas kernels, local_step(): pl.pallas_call(kernel, out_shape=jax.ShapeDtypeStruct((BATCH, 2, LATENT),...  71.3 us

profile of v8, /device:TPU:1, one launch (start us, length us, event | category | flops | bytes accessed | tf_op | source)
XLA Modules:
  0.0 72.0 jit_solution(1791528040030540879)
XLA Ops:
  0.0 71.3 %mla.1 = bf16[64,2,512]{2,1,0:T(2,128)(2,1)S(1)} custom-call(s32[64]{0:T(128)} %len_hbm.1, bf16[64,2,576]{2,1,0:T(2,128)(2,1)} %bitcast.5, bf16[64,2,1,64,576]{4,3,2,1,0:T(8,128)(2,1)} %kv_ref.1), custom_call_target="tpu_custom_call" | custom-call | tf_op jit(solution)/shard_map/mla/pallas_call | solution.py:354
  71.3 0.7 copy.6

commit v9 on v8

--- a/solution.py
+++ b/solution.py
@@ -252,8 +252,7 @@
         zero = jnp.zeros_like(packed)
         rope = jnp.stack([jnp.where(lane < ROPE, packed, zero), jnp.where(lane >= ROPE, packed, zero)], axis=1).reshape(1024, 2 * ROPE)
         nt = (((1,), (1,)), ((), ()))
-        s = lax.dot_general(q, keys, nt, preferred_element_type=F32)
-        s = s + lax.dot_general(qr, rope, nt, preferred_element_type=F32)
+        s = lax.dot_general(jnp.concatenate([q, qr], axis=1), jnp.concatenate([keys, rope], axis=1), nt, preferred_element_type=F32)
         s = s * SCALE
         kk = lax.broadcasted_iota(jnp.int32, (1, 1024), 1)
         dsrc = (me - u * ring - core) + (kk >> 8) * ring + ((kk >> 7) & 1)

time: 72.1 us -> 72.1 us (level)
  no operation moved by 1% of the time
where the time goes in v9:
time: 72.1 us; the launch traced here: 72 us
  Pallas kernels  71.3 us (99%)
    pallas_call x1, Pallas kernels, local_step(): pl.pallas_call(kernel, out_shape=jax.ShapeDtypeStruct((BATCH, 2, LATENT),...  71.3 us

profile of v9, /device:TPU:1, one launch (start us, length us, event | category | flops | bytes accessed | tf_op | source)
XLA Modules:
  0.0 72.0 jit_solution(2992245096793004139)
XLA Ops:
  0.0 71.3 %mla.1 = bf16[64,2,512]{2,1,0:T(2,128)(2,1)S(1)} custom-call(s32[64]{0:T(128)} %len_hbm.1, bf16[64,2,576]{2,1,0:T(2,128)(2,1)} %bitcast.5, bf16[64,2,1,64,576]{4,3,2,1,0:T(8,128)(2,1)} %kv_ref.1), custom_call_target="tpu_custom_call" | custom-call | tf_op jit(solution)/shard_map/mla/pallas_call | solution.py:353
  71.3 0.7 copy.6

commit v10 on v9

--- a/solution.py
+++ b/solution.py
@@ -103,8 +103,9 @@
 
 def kernel(len_hbm, q_ref, kv_ref, out_ref, len_ref, qlocal, kvlocal, ropes, kvbuf, kvrope, qsend, q0buf, qbuf, obuf, r1buf, m1buf, r2buf,
            l1send, l1recv, l2send, l2recv, tally, fsend, frecv,
-           len_s, ql_s, loc_s, kv_s, kv_r, kv_l, kr_s, kr_r, q0_s, q0_r, q1_s, q1_r, q2_s, q2_r, q3_s, q3_r, r1_s, r1_r, r2_s, r2_r,
-           l1_s, l2_s, f_s, f_r):
+           all_s,
+           len_s, ql_s, loc_s, kv_s, kv_r, kv_l, kr_r, q0_s, q0_r, q1_r, q2_r, q3_r, r1_r, r2_r,
+           f_r):
     me = lax.axis_index('dcp')
     core = lax.rem(me, 2)
     queries = pltpu.make_async_copy(q_ref, qlocal, ql_s)
@@ -173,7 +174,7 @@
         view = qbuf.at[k, pl.ds(i, n), big[k], small[k]]
         for d in STEPS:
             dev = shifted(me, SMALL[k] if last_big else BIG[k], d)
-            remote(view, view, q1_s, q1_r.at[j], dev).start()
+            remote(view, view, all_s, q1_r.at[j], dev).start()
     for t in range(2):
         send_cache(t, far)
 
@@ -189,7 +190,7 @@
         arrived(block(u, 0, 0, 3), q1_r.at[u])
         view = block(u, mid[u], 0, 4)
         for j, d in enumerate(STEPS[:2]):
-            remote(view, view, q2_s, q2_r.at[u, j], shifted(me, axis[u], d)).start()
+            remote(view, view, all_s, q2_r.at[u, j], shifted(me, axis[u], d)).start()
     local.wait()
     def pack(b, carry):
         ropes[b] = jnp.concatenate([kvlocal[b, 0, :, pl.ds(LATENT, ROPE)], kvlocal[b, 1, :, pl.ds(LATENT, ROPE)]], axis=1)
@@ -200,7 +201,7 @@
         n = COUNT[k]
         for d, flip in others:
             dev, o = ring_dest(k, d, flip)
-            remote(ropes.at[pl.ds(BASE[k] + o * n, n)], kvrope.at[k, own[k], first(n)], kr_s, kr_r, dev).start()
+            remote(ropes.at[pl.ds(BASE[k] + o * n, n)], kvrope.at[k, own[k], first(n)], all_s, kr_r, dev).start()
         kvrope[k, own[k], first(n)] = ropes[pl.ds(BASE[k] + own[k] * n, n)]
 
     send_cache(3, others)
@@ -211,7 +212,7 @@
         for j, d in enumerate(STEPS[:2]):
             arrived(block(k, mid[k], 0, 4), q2_r.at[k, j])
             half = block(k, lax.rem(mid[k] + (3 if j == 0 else 1), 4), 2 * j, 2)
-            remote(half, half, q3_s, q3_r.at[k], shifted(me, axis[k], d)).start()
+            remote(half, half, all_s, q3_r.at[k], shifted(me, axis[k], d)).start()
     forward(2)
     send_cache(4, others[2:])
     send_cache(6, others)
@@ -271,8 +272,8 @@
         for d in SENDS:
             b = lax.rem(b_me + d, 4)
             dev = me + (b - b_me) * bstride
-            remote(obuf.at[k, i, b], r1buf.at[t, b_me], r1_s, r1_r.at[t], dev).start()
-            remote(l1send.at[k, i, b], l1recv.at[t, b_me], l1_s, r1_r.at[t], dev).start()
+            remote(obuf.at[k, i, b], r1buf.at[t, b_me], all_s, r1_r.at[t], dev).start()
+            remote(l1send.at[k, i, b], l1recv.at[t, b_me], all_s, r1_r.at[t], dev).start()
         r1buf[t, b_me] = obuf[k, i, b_me]
         l1recv[t, b_me] = l1send[k, i, b_me]
         return carry
@@ -298,13 +299,13 @@
         lacc[k] = put_lse(lacc[k], lse, i)
         for d in SENDS:
             b = lax.rem(small[k] + d, 4)
-            remote(m1buf.at[k, i, b], r2buf.at[t, small[k]], r2_s, r2_r.at[k], shifted(me, SMALL[k], d)).start()
+            remote(m1buf.at[k, i, b], r2buf.at[t, small[k]], all_s, r2_r.at[k], shifted(me, SMALL[k], d)).start()
         r2buf[t, small[k]] = m1buf[k, i, small[k]]
         if i == COUNT[k] - 1:
             l2send[k] = lacc[k].astype(BF16)
             for d in SENDS:
                 b = lax.rem(small[k] + d, 4)
-                remote(l2send.at[k, b], l2recv.at[k, small[k]], l2_s, r2_r.at[k], shifted(me, SMALL[k], d)).start()
+                remote(l2send.at[k, b], l2recv.at[k, small[k]], all_s, r2_r.at[k], shifted(me, SMALL[k], d)).start()
             l2recv[k, small[k]] = l2send[k, small[k]]
 
     for k in (0, 2, 1):
@@ -320,7 +321,7 @@
         fsend[k] = out.astype(BF16).reshape(8, 8, LATENT)
         for d, flip in far + near:
             dev, o = ring_dest(k, d, flip)
-            remote(fsend.at[k, o], frecv.at[k, own[k]], f_s, f_r, dev).start()
+            remote(fsend.at[k, o], frecv.at[k, own[k]], all_s, f_r, dev).start()
         frecv[k, own[k]] = fsend[k, own[k]]
     back = onehot((128, 192), lambda r, c: by_set(c, r, 8, 2, 0))
     arrived(frecv.at[:, first(7)], f_r)
@@ -329,17 +330,9 @@
     def sent(view, sem):
         remote(view, view, sem, sem, me).wait_send()
 
+    sent(tally, all_s)
     sent(q0buf.at[:, first(7)], q0_s)
-    sent(qbuf.at[first(2), :, :, 0], q1_s)
-    sent(qbuf.at[first(2), first(2)], q2_s)
-    sent(qbuf.at[first(2), 0], q3_s)
-    sent(ropes.at[first(56)], kr_s)
     sent(kvbuf.at[:, first(7)], kv_s)
-    sent(r1buf.at[first(SLOTS), first(3)], r1_s)
-    sent(l1recv.at[first(SLOTS), first(3)], l1_s)
-    sent(r2buf.at[first(SLOTS), first(3)], r2_s)
-    sent(l2recv.at[:, first(3)], l2_s)
-    sent(frecv.at[:, first(7)], f_s)
 
 
 def solution(mesh):
@@ -377,20 +370,20 @@
                 vmem((SLOTS, 4, 16, 128), BF16),
                 vmem((3, 4, 16, 128), BF16),
                 vmem((3, 4, 16, 128), BF16),
-                vmem((51, 16, 128), BF16),
+                vmem((1319, 16, 128), BF16),
                 vmem((3, 8, 8, LATENT), BF16),
                 vmem((3, 8, 8, LATENT), BF16),
+                dma,
                 dma, dma, dma,
                 dma, dma((SLOTS,)), dma,
+                dma,
                 dma, dma,
-                dma, dma,
-                dma, dma((3,)),
-                dma, dma((3, 2)),
-                dma, dma((3,)),
-                dma, dma((SLOTS,)),
-                dma, dma((3,)),
-                dma, dma,
-                dma, dma,
+                dma((3,)),
+                dma((3, 2)),
+                dma((3,)),
+                dma((SLOTS,)),
+                dma((3,)),
+                dma,
             ],
             compiler_params=pltpu.CompilerParams(collective_id=0, has_side_effects=True, vmem_limit_bytes=44 * 1024 * 1024),
             name='mla',

time: 72.1 us -> 72 us (level)
  no operation moved by 1% of the time
where the time goes in v10:
time: 72 us; the launch traced here: 71.9 us
  Pallas kernels  71.2 us (99%)
    pallas_call x1, Pallas kernels, local_step(): pl.pallas_call(kernel, out_shape=jax.ShapeDtypeStruct((BATCH, 2, LATENT),...  71.2 us

profile of v10, /device:TPU:1, one launch (start us, length us, event | category | flops | bytes accessed | tf_op | source)
XLA Modules:
  0.0 71.9 jit_solution(5879250644262117292)
XLA Ops:
  0.0 71.2 %mla.1 = bf16[64,2,512]{2,1,0:T(2,128)(2,1)S(1)} custom-call(s32[64]{0:T(128)} %len_hbm.1, bf16[64,2,576]{2,1,0:T(2,128)(2,1)} %bitcast.5, bf16[64,2,1,64,576]{4,3,2,1,0:T(8,128)(2,1)} %kv_ref.1), custom_call_target="tpu_custom_call" | custom-call | tf_op jit(solution)/shard_map/mla/pallas_call | solution.py:346
  71.2 0.7 copy.6
